TPU v7x, 32 devices: a whole 2x2x4 slice. The times are simulated.
32 devices in a mesh: groups: 2 (over y), seq: 4 (over z), tensor: 2 (over x), cfg: 2 (over core).
Axes of the slice: x: 2, y: 2, z: 4, core: 2. Of those that a mesh axis runs over, the one named last changes fastest.
Arguments:
- latent: bfloat16 [2048, 3072], P(('groups', 'seq')), parts along dimension 0, may hold values from -6 to 6
- positions: int32 [3, 2048], P(None, ('groups', 'seq')), parts along dimension 1, may hold values from 0 to 79, as said below
- text_kv: bfloat16 [2, 2, 128, 3072], P('cfg', None, ('groups', 'seq'), 'tensor'), parts along dimension 2, may hold values from -6 to 6
- text_len: int32 [4], P(('groups', 'cfg')), parts along dimension 0, may hold values from 1 to 64
- modulation: float32 [3, 4, 3072], P(None, 'groups'), parts along dimension 1, may hold values from -3 to 3
- w_qkv: bfloat16 [3, 3072, 3072], P(None, 'cfg', 'tensor'), may hold values from -0.109375 to 0.109375
- norm_gains: float32 [2, 128], replicated, may hold values from 0.5 to 2.5
- w_out: bfloat16 [3072, 3072], P('tensor', 'cfg'), may hold values from -0.109375 to 0.109375
- guidance: float32 [2], P('groups'), parts along dimension 0, may hold values from 3 to 8
Outputs:
- guided: bfloat16 [2048, 3072], P(('groups', 'seq', 'tensor'), 'cfg'), parts along dimension 0
There are 2 independent parts, one for each index of `groups`. A program takes and returns all parts, laid end to end along the dimension named above; an argument that names none is the same for every part. Nothing has to cross between parts.
Inputs may be any that keep to these rules, and one draw needn't show every extreme that they name: `positions`: frame indices are below 33, height indices below 45, width indices below 80. `text_len`: text rows at or beyond the count are ignored.
All inputs are finite; a program needn't handle non-finite values.
Results may differ from a plain program's by a relative error of at most 0.018.
Values may be sent and summed in bfloat16 or wider, within the bound.
A program may use at most 128 MiB of HBM per device.

v0:
```python
import functools

import jax
import jax.numpy as jnp
import numpy as np
from jax import lax
from jax.experimental import pallas as pl
from jax.experimental.pallas import tpu as pltpu
from jax.sharding import PartitionSpec as P

HEAD_DIM = 128
MESH = pl.DeviceIdType.MESH
U_TILE = True
U_MOD = 8
U_ATT = 4
U_TEXT = 2
F32 = jnp.float32
BF16 = jnp.bfloat16


def rotary_rows(head_size):
    rows = np.zeros((8, head_size), np.float32)
    axes = np.zeros((head_size,), np.int32)
    blocks = (head_size // 8, 7 * head_size // 16, 7 * head_size // 16)
    halves = []
    offset = 0
    for axis_id, width in enumerate(blocks):
        half = width // 2
        if half not in halves:
            halves.append(half)
        which = halves.index(half)
        freq = (256.0 ** (-np.arange(half, dtype=np.float64) / half)).astype(np.float32)
        rows[0, offset : offset + half] = freq
        rows[0, offset + half : offset + width] = freq
        rows[1 + 2 * which, offset : offset + half] = -1.0
        rows[2 + 2 * which, offset + half : offset + width] = 1.0
        axes[offset : offset + width] = axis_id
        offset += width
    shifts = []
    for half in halves:
        shifts += [head_size - half, half]
    return rows, axes, tuple(shifts)


ROT_ROWS, ROT_AXES, ROT_SHIFTS = rotary_rows(HEAD_DIM)
ROT_PICK = (np.arange(16)[:, None] == ROT_AXES[None, :]).astype(np.float32)


def kernel(
    seq_n,
    ten_n,
    latent,
    pos_in,
    text_kv,
    lens_in,
    modulation,
    w_qkv,
    gains,
    w_out,
    guide,
    rot,
    pick,
    out,
    lat,
    pos,
    txt,
    lens,
    wfull,
    wout,
    mod,
    tab,
    qbuf,
    kbuf,
    vbuf,
    acc,
    lsum,
    attf,
    part,
    got,
    send_a,
    recv_a,
    send_b,
    recv_b,
    send_c,
    recv_c,
    send_p,
    recv_p,
    send_t,
    recv_t,
    send_w,
    recv_w,
    send_l,
    recv_l,
    send_o,
    recv_o,
    send_r,
    recv_r,
    loc,
):
    x = lax.axis_index("tensor")
    c = lax.axis_index("cfg")
    z = lax.axis_index("seq")
    other = 1 - c
    rows, width = latent.shape
    half = w_qkv.shape[1]
    mine = wfull.shape[2]
    heads = mine // HEAD_DIM
    half_rows = rows // 2
    piece = half_rows // ten_n
    out_rows = rows // ten_n
    out_cols = w_out.shape[1]
    scale = HEAD_DIM ** (-0.5)
    tile = 256 if mine % 256 == 0 else 128
    per_tile = tile // HEAD_DIM
    shorter = jnp.minimum(z, seq_n - 1 - z)
    long_sign = jnp.where(2 * z < seq_n - 1, 1, -1)

    def order(i):
        near = i <= 2 * shorter
        dist = jnp.where(near, (i + 1) // 2, i - shorter)
        sign = jnp.where(near, 2 * (i % 2) - 1, long_sign)
        return jnp.where(i == 0, z, z + dist * sign)

    def remote(src, dst, send, recv, **to):
        return pltpu.make_async_remote_copy(
            src_ref=src, dst_ref=dst, send_sem=send, recv_sem=recv, device_id=to, device_id_type=MESH
        )

    def aligned(value, unit):
        return pl.multiple_of(value * unit, unit)

    cols_of = lambda core: pl.ds(aligned(core, mine), mine)
    w_copy = [
        remote(
            w_qkv.at[j, :, cols_of(other)],
            wfull.at[j, pl.ds(aligned(c, half), half), :],
            send_w.at[j],
            recv_w.at[j],
            cfg=other,
        )
        for j in range(3)
    ]
    w_local = [
        pltpu.make_async_copy(
            w_qkv.at[j, :, cols_of(c)], wfull.at[j, pl.ds(aligned(c, half), half), :], loc.at[j]
        )
        for j in range(3)
    ]
    lat_local = pltpu.make_async_copy(latent, lat.at[z], loc.at[3])
    pos_local = pltpu.make_async_copy(pos_in, pos.at[z], loc.at[4])
    txt_local = pltpu.make_async_copy(text_kv.at[0, :, :, cols_of(c)], txt.at[c, z], loc.at[5])
    len_local = pltpu.make_async_copy(lens_in, lens.at[c], loc.at[6])
    out_local = pltpu.make_async_copy(w_out, wout, loc.at[7])
    my_piece = pl.ds(pl.multiple_of((c * ten_n + x) * piece, piece), piece)

    def copy_a(i):
        return remote(
            latent.at[my_piece], lat.at[z, my_piece], send_a.at[i], recv_a.at[z], seq=order(i)
        )

    def arrived_a(o):
        return remote(
            latent.at[my_piece], lat.at[o, my_piece], send_a.at[0], recv_a.at[o], seq=order(1)
        )

    def copy_b(o, t):
        to = (x + t) % ten_n
        return remote(
            lat.at[o, my_piece], lat.at[o, my_piece], send_b.at[o, t], recv_b.at[o, t], tensor=to
        )

    def arrived_b(o, t):
        source = (x + ten_n - t) % ten_n
        landed = pl.ds(pl.multiple_of((c * ten_n + source) * piece, piece), piece)
        return remote(
            lat.at[o, landed], lat.at[o, landed], send_b.at[o, t], recv_b.at[o, t], tensor=source
        )

    def copy_c(o, core):
        at = pl.ds(aligned(core, half_rows), half_rows)
        return remote(lat.at[o, at], lat.at[o, at], send_c.at[o], recv_c.at[o], cfg=other)

    def copy_p(i):
        return remote(pos_in, pos.at[z], send_p.at[i], recv_p.at[z], seq=order(i))

    def arrived_p(o):
        return remote(pos_in, pos.at[o], send_p.at[0], recv_p.at[o], seq=order(1))

    def copy_t(i, core):
        return remote(
            text_kv.at[0, :, :, cols_of(core)],
            txt.at[c, z],
            send_t.at[core, i],
            recv_t.at[c, z],
            seq=order(i),
            cfg=core,
        )

    def copy_t_mirror():
        return remote(
            text_kv.at[0, :, :, cols_of(other)],
            txt.at[c, z],
            send_t.at[other, 0],
            recv_t.at[c, z],
            cfg=other,
        )

    def arrived_t(core, o):
        return remote(
            text_kv.at[0, :, :, cols_of(c)], txt.at[core, o], send_t.at[c, 0], recv_t.at[core, o], cfg=other
        )

    def copy_l(core):
        return remote(lens_in, lens.at[core], send_l.at[0], recv_l.at[0], cfg=other)

    for j in range(3):
        w_local[j].start()
    lat_local.start()
    pos_local.start()
    txt_local.start()
    len_local.start()
    out_local.start()

    barrier = pltpu.get_barrier_semaphore()
    pl.semaphore_signal(barrier, inc=1, device_id={"cfg": other}, device_id_type=MESH)
    for t in range(1, ten_n):
        pl.semaphore_signal(
            barrier, inc=1, device_id={"tensor": (x + t) % ten_n}, device_id_type=MESH
        )
    for s in range(1, seq_n):
        for k in range(2):
            pl.semaphore_signal(
                barrier,
                inc=1,
                device_id={"seq": (z + s) % seq_n, "cfg": (c + k) % 2},
                device_id_type=MESH,
            )
    pl.semaphore_wait(barrier, 1 + (ten_n - 1) + 2 * (seq_n - 1))

    for j in range(3):
        w_copy[j].start()

    @pl.loop(1, seq_n)
    def _(i):
        copy_p(i).start()
        copy_a(i).start()

    copy_l(c).start()
    copy_t_mirror().start()

    @pl.loop(1, seq_n)
    def _(i):
        copy_t(i, 0).start()
        copy_t(i, 1).start()

    acc[...] = jnp.zeros_like(acc)
    lsum[...] = jnp.zeros_like(lsum)
    lat_local.wait()
    pos_local.wait()

    def pump_a(i):
        o = order(i)
        arrived_a(o).wait_recv()
        for t in range(1, ten_n):
            copy_b(o, t).start()

    def pump_b(i):
        o = order(i)
        for t in range(1, ten_n):
            arrived_b(o, t).wait_recv()
        copy_c(o, c).start()

    def normed_head(value, gain):
        return (
            value * lax.rsqrt(jnp.mean(value * value, axis=-1, keepdims=True) + 1e-06) * gain
        )

    def turned(value):
        total = value * tab[0]
        for k, shift in enumerate(ROT_SHIFTS):
            total = total + pltpu.roll(value, shift, 1) * tab[1 + k]
        return total

    def project(j, t):
        at = pl.ds(pl.multiple_of(t * tile, tile), tile)
        return [
            jnp.dot(mod[b * rows : (b + 1) * rows, :], wfull[j, :, at], preferred_element_type=F32)
            for b in range(2)
        ]

    def head_tiles(j, gain_row, dest):
        @pl.loop(0, mine // tile, unroll=U_TILE)
        def _(t):
            y = project(j, t)
            gain = gains[gain_row : gain_row + 1, :]
            for hh in range(per_tile):
                for b in range(2):
                    part_in = y[b][:, hh * HEAD_DIM : (hh + 1) * HEAD_DIM]
                    dest[b * heads + t * per_tile + hh] = turned(normed_head(part_in, gain)).astype(
                        BF16
                    )

    def value_tiles():
        @pl.loop(0, mine // tile, unroll=U_TILE)
        def _(t):
            y = [value.astype(BF16) for value in project(2, t)]
            for hh in range(per_tile):
                for b in range(2):
                    vbuf[b * heads + t * per_tile + hh] = y[b][:, hh * HEAD_DIM : (hh + 1) * HEAD_DIM]

    strip = 16

    @pl.loop(0, seq_n)
    def _(i):
        o = order(i)

        @pl.when(i > 0)
        def _():
            arrived_p(o).wait_recv()
            copy_c(o, other).wait_recv()

        place = lax.dot_general(
            pos[o], pick[...], (((0,), (0,)), ((), ())), preferred_element_type=F32
        )
        angle = place * rot[0:1, :]
        sine = jnp.sin(angle)
        tab[0] = jnp.cos(angle)
        for k in range(len(ROT_SHIFTS)):
            tab[1 + k] = sine * rot[1 + k : 2 + k, :]

        @pl.loop(0, rows // strip, unroll=U_MOD)
        def _(r):
            at = pl.ds(pl.multiple_of(r * strip, strip), strip)
            value = lat[o, at, :].astype(F32)
            center = value - jnp.mean(value, axis=-1, keepdims=True)
            normed = center * lax.rsqrt(jnp.mean(center * center, axis=-1, keepdims=True) + 1e-06)
            for b in range(2):
                mod[pl.ds(pl.multiple_of(b * rows + r * strip, strip), strip), :] = (
                    normed * (1.0 + modulation[1, b : b + 1, :]) + modulation[0, b : b + 1, :]
                ).astype(BF16)

        @pl.when(i == 0)
        def _():
            w_local[0].wait()
            w_copy[0].wait_recv()
            head_tiles(0, 0, qbuf)
            w_local[1].wait()
            w_copy[1].wait_recv()
            if seq_n > 1:
                pump_a(1)

        head_tiles(1, 1, kbuf)

        @pl.when(i == 0)
        def _():
            w_local[2].wait()
            w_copy[2].wait_recv()

        value_tiles()

        @pl.when(i + 1 < seq_n)
        def _():
            pump_b(i + 1)

        @pl.loop(0, 2 * heads, unroll=U_ATT)
        def _(h):
            scores = lax.dot_general(
                qbuf[h], kbuf[h], (((1,), (1,)), ((), ())), preferred_element_type=F32
            )
            expo = jnp.exp(scores * scale)
            folded = expo[:, :HEAD_DIM]
            for k in range(1, rows // HEAD_DIM):
                folded = folded + expo[:, k * HEAD_DIM : (k + 1) * HEAD_DIM]
            lsum[h] += folded
            acc[h] += jnp.dot(expo.astype(BF16), vbuf[h], preferred_element_type=F32)

        @pl.when(i + 2 < seq_n)
        def _():
            pump_a(i + 2)

    txt_local.wait()
    len_local.wait()
    copy_l(other).wait_recv()
    arrived_t(other, z).wait_recv()

    @pl.loop(1, seq_n)
    def _(i):
        arrived_t(0, order(i)).wait_recv()
        arrived_t(1, order(i)).wait_recv()

    text_rows = txt.shape[3]
    count = seq_n * text_rows
    for b in range(2):
        valid = lax.broadcasted_iota(jnp.int32, (1, count), 1).astype(F32) < lens[b, 0:1, :]

        @pl.loop(0, heads, unroll=U_TEXT)
        def _(h):
            at = pl.ds(pl.multiple_of(h * HEAD_DIM, HEAD_DIM), HEAD_DIM)
            raw = txt[b, :, 0, :, at].reshape(count, HEAD_DIM).astype(F32)
            keys = normed_head(raw, gains[1:2, :]).astype(BF16)
            values = txt[b, :, 1, :, at].reshape(count, HEAD_DIM)
            n = b * heads + h
            scores = lax.dot_general(
                qbuf[n], keys, (((1,), (1,)), ((), ())), preferred_element_type=F32
            )
            expo = jnp.where(valid, jnp.exp(scores * scale), 0.0)
            total = jnp.sum(lsum[n], axis=-1, keepdims=True) + jnp.sum(
                expo, axis=-1, keepdims=True
            )
            mixed = acc[n] + jnp.dot(expo.astype(BF16), values, preferred_element_type=F32)
            attf[c, b, :, at] = (mixed / total).astype(BF16)

    def copy_o(core):
        return remote(attf.at[core], attf.at[core], send_o.at[0], recv_o.at[0], cfg=other)

    copy_o(c).start()
    out_local.wait()
    copy_o(other).wait_recv()

    def copy_r(t):
        return remote(part.at[t], got.at[t], send_r.at[t], recv_r.at[t], tensor=(x + t) % ten_n)

    out_tile = 256 if out_cols % 256 == 0 else 128

    def out_block(t, k, at):
        to = (x + t) % ten_n
        here = pl.ds(pl.multiple_of(to * out_rows, out_rows), out_rows)
        total = None
        strength = guide[0:1, 0:1]
        at_gate = pl.ds(pl.multiple_of(c * out_cols + k * out_tile, out_tile), out_tile)
        gates = (
            strength * modulation[2, 0:1, at_gate],
            (1.0 - strength) * modulation[2, 1:2, at_gate],
        )
        for b in range(2):
            y = jnp.dot(attf[0, b, here, :], wout[0:mine, at], preferred_element_type=F32)
            y = y + jnp.dot(
                attf[1, b, here, :], wout[mine : 2 * mine, at], preferred_element_type=F32
            )
            y = y * gates[b]
            total = y if total is None else total + y
        return total

    for t in range(1, ten_n):

        @pl.loop(0, out_cols // out_tile)
        def _(k):
            at = pl.ds(pl.multiple_of(k * out_tile, out_tile), out_tile)
            part[t, :, at] = out_block(t, k, at).astype(BF16)

        copy_r(t).start()


    @pl.loop(0, out_cols // out_tile)
    def _(k):
        at = pl.ds(pl.multiple_of(k * out_tile, out_tile), out_tile)
        part[0, :, at] = out_block(0, k, at).astype(BF16)

    for t in range(1, ten_n):
        copy_r(t).wait_recv()
    total = part[0].astype(F32)
    for t in range(1, ten_n):
        total = total + got[t].astype(F32)
    out[...] = total.astype(BF16)

    for j in range(3):
        w_copy[j].wait_send()
    copy_l(c).wait_send()
    copy_t_mirror().wait_send()
    copy_o(c).wait_send()
    for t in range(1, ten_n):
        copy_r(t).wait_send()

    @pl.loop(1, seq_n)
    def _(i):
        copy_p(i).wait_send()
        copy_a(i).wait_send()
        copy_t(i, 0).wait_send()
        copy_t(i, 1).wait_send()
        o = order(i)
        for t in range(1, ten_n):
            copy_b(o, t).wait_send()
        copy_c(o, c).wait_send()


def local(
    seq_n, ten_n, latent, positions, text_kv, text_len, modulation, w_qkv, norm_gains, w_out, guidance
):
    rows, width = latent.shape
    mine = w_qkv.shape[2] // 2
    heads = mine // HEAD_DIM
    text_dev = text_kv.shape[2]
    out_rows = rows // ten_n
    out_cols = w_out.shape[1]
    pos_in = jnp.pad(positions.astype(BF16), ((0, 13), (0, 0)))
    lens = jnp.broadcast_to(text_len.astype(F32)[None, :], (8, seq_n * text_dev))
    any_space = pl.BlockSpec(memory_space=pl.ANY)
    vmem = pl.BlockSpec(memory_space=pltpu.VMEM)
    dma = pltpu.SemaphoreType.DMA
    return pl.pallas_call(
        functools.partial(kernel, seq_n, ten_n),
        out_shape=jax.ShapeDtypeStruct((out_rows, out_cols), BF16),
        in_specs=[
            any_space,
            any_space,
            any_space,
            any_space,
            vmem,
            any_space,
            vmem,
            any_space,
            vmem,
            vmem,
            vmem,
        ],
        out_specs=vmem,
        scratch_shapes=[
            pltpu.VMEM((seq_n, rows, width), BF16),
            pltpu.VMEM((seq_n, 16, rows), BF16),
            pltpu.VMEM((2, seq_n, 2, text_dev, mine), BF16),
            pltpu.VMEM((2, 8, seq_n * text_dev), F32),
            pltpu.VMEM((3, width, mine), BF16),
            pltpu.VMEM(w_out.shape, BF16),
            pltpu.VMEM((2 * rows, width), BF16),
            pltpu.VMEM((1 + len(ROT_SHIFTS), rows, HEAD_DIM), F32),
            pltpu.VMEM((2 * heads, rows, HEAD_DIM), BF16),
            pltpu.VMEM((2 * heads, rows, HEAD_DIM), BF16),
            pltpu.VMEM((2 * heads, rows, HEAD_DIM), BF16),
            pltpu.VMEM((2 * heads, rows, HEAD_DIM), F32),
            pltpu.VMEM((2 * heads, rows, HEAD_DIM), F32),
            pltpu.VMEM((2, 2, rows, mine), BF16),
            pltpu.VMEM((ten_n, out_rows, out_cols), BF16),
            pltpu.VMEM((ten_n, out_rows, out_cols), BF16),
            dma((seq_n,)),
            dma((seq_n,)),
            dma((seq_n, ten_n)),
            dma((seq_n, ten_n)),
            dma((seq_n,)),
            dma((seq_n,)),
            dma((seq_n,)),
            dma((seq_n,)),
            dma((2, seq_n)),
            dma((2, seq_n)),
            dma((3,)),
            dma((3,)),
            dma((1,)),
            dma((1,)),
            dma((1,)),
            dma((1,)),
            dma((ten_n,)),
            dma((ten_n,)),
            dma((8,)),
        ],
        compiler_params=pltpu.CompilerParams(
            collective_id=0, has_side_effects=True, vmem_limit_bytes=64 * 1024 * 1024 - 65536
        ),
    )(
        latent,
        pos_in,
        text_kv,
        lens,
        modulation,
        w_qkv,
        norm_gains,
        w_out,
        guidance.reshape(1, 1),
        jnp.asarray(ROT_ROWS),
        jnp.asarray(ROT_PICK, BF16),
    )


def solution(mesh):
    placed = (
        P(("groups", "seq"), None),
        P(None, ("groups", "seq")),
        P("cfg", None, ("groups", "seq"), "tensor"),
        P(("groups", "cfg")),
        P(None, "groups", None),
        P(None, "cfg", "tensor"),
        P(),
        P("tensor", "cfg"),
        P("groups"),
    )
    return jax.shard_map(
        functools.partial(local, mesh.shape["seq"], mesh.shape["tensor"]),
        mesh=mesh,
        in_specs=placed,
        out_specs=P(("groups", "seq", "tensor"), "cfg"),
        check_vma=False,
    )
```

profile of v0, /device:TPU:0, one launch (start us, length us, event | category | flops | bytes accessed | tf_op | source)
XLA Modules:
  0.0 104.6 jit_solution(14339253362111551334)
XLA Ops:
  1.3 0.7 convert_element_type.8
  2.0 0.6 broadcast_in_dim.9.lens_in
  2.6 0.6 pad.4.pos_in
  3.2 99.7 %shard_map.109 = bf16[128,1536]{1,0:T(8,128)(2,1)} custom-call(bf16[256,3072]{1,0:T(8,128)(2,1)} %latent.1, bf16[16,256]{1,0:T(8,128)(2,1)} %pad.4.pos_in, bf16[1,2,16,1536]{3,2,1,0:T(8,128)(2,1)} %text_kv.1, f32[8,64]{1,0:T(8,128)} %broadcast_in_dim.9.lens_in, f32[3,2,3072]{2,1,0:T(2,128)} %modulation.1, bf16[3,1536,1536]{2,1,0:T(8,128)(2,1)} %w_qkv.1, ...), custom_call_target="tpu_custom_call" | custom-call | tf_op jit(solution)/shard_map/pallas_call | solution.py:500
  102.9 1.8 %copy.15 = bf16[128,1536]{1,0:T(8,128)(2,1)} copy(bf16[128,1536]{1,0:T(8,128)(2,1)} %shard_map.109) | data formatting | bytes 786432
where the time goes:
time: 105 us
  Pallas kernels  99.7 us (95%)
  local copies, waits for them, and re-layouts  2.95 us (3%)
  between operations  1.31 us (1%)
    pallas_call x1, Pallas kernels, local(): pl.pallas_call(functools.partial(kernel, seq_n, ten_n), out_shape=jax.Sha...  99.7 us

commit v1 on v0

v1 whole, which is shorter than its diff:
```python
import functools

import jax
import jax.numpy as jnp
import numpy as np
from jax import lax
from jax.experimental import pallas as pl
from jax.experimental.pallas import tpu as pltpu
from jax.sharding import PartitionSpec as P

HEAD_DIM = 128
MESH = pl.DeviceIdType.MESH
U_TILE = True
U_MOD = 8
U_ATT = 4
U_TEXT = 2
F32 = jnp.float32
BF16 = jnp.bfloat16


def rotary_rows(head_size):
    rows = np.zeros((8, head_size), np.float32)
    axes = np.zeros((head_size,), np.int32)
    blocks = (head_size // 8, 7 * head_size // 16, 7 * head_size // 16)
    halves = []
    offset = 0
    for axis_id, width in enumerate(blocks):
        half = width // 2
        if half not in halves:
            halves.append(half)
        which = halves.index(half)
        freq = (256.0 ** (-np.arange(half, dtype=np.float64) / half)).astype(np.float32)
        rows[0, offset : offset + half] = freq
        rows[0, offset + half : offset + width] = freq
        rows[1 + 2 * which, offset : offset + half] = -1.0
        rows[2 + 2 * which, offset + half : offset + width] = 1.0
        axes[offset : offset + width] = axis_id
        offset += width
    shifts = []
    for half in halves:
        shifts += [head_size - half, half]
    return rows, axes, tuple(shifts)


ROT_ROWS, ROT_AXES, ROT_SHIFTS = rotary_rows(HEAD_DIM)
ROT_PICK = (np.arange(16)[:, None] == ROT_AXES[None, :]).astype(np.float32)


STRIP = 16


def kernel(
    seq_n,
    ten_n,
    latent,
    pos_in,
    text_kv,
    lens_in,
    modulation,
    w_qkv,
    gains,
    w_out,
    guide,
    rot,
    pick,
    out,
    lat,
    pos,
    txt,
    txo,
    lens,
    wfull,
    wout,
    mod,
    tab,
    qbuf,
    kbuf,
    vbuf,
    acc,
    lsum,
    attf,
    part,
    got,
    send_a,
    recv_a,
    send_b,
    recv_b,
    send_c,
    recv_c,
    send_p,
    recv_p,
    send_t,
    recv_t,
    send_u,
    recv_u,
    send_w,
    recv_w,
    send_l,
    recv_l,
    send_o,
    recv_o,
    send_r,
    recv_r,
    loc,
):
    x = lax.axis_index("tensor")
    c = lax.axis_index("cfg")
    z = lax.axis_index("seq")
    other = 1 - c
    rows, width = latent.shape
    half = w_qkv.shape[1]
    mine = wfull.shape[2]
    heads = mine // HEAD_DIM
    half_rows = rows // 2
    band = ten_n * STRIP
    subs = half_rows // band
    out_rows = rows // ten_n
    out_cols = w_out.shape[1]
    scale = HEAD_DIM ** (-0.5)
    tile = 256 if mine % 256 == 0 else 128
    per_tile = tile // HEAD_DIM
    tiles = mine // tile
    shorter = jnp.minimum(z, seq_n - 1 - z)
    long_sign = jnp.where(2 * z < seq_n - 1, 1, -1)

    def order(i):
        near = i <= 2 * shorter
        dist = jnp.where(near, (i + 1) // 2, i - shorter)
        sign = jnp.where(near, 2 * (i % 2) - 1, long_sign)
        return jnp.where(i == 0, z, z + dist * sign)

    def remote(src, dst, send, recv, **to):
        return pltpu.make_async_remote_copy(
            src_ref=src, dst_ref=dst, send_sem=send, recv_sem=recv, device_id=to, device_id_type=MESH
        )

    def aligned(value, unit):
        return pl.multiple_of(value * unit, unit)

    def inside(o):
        return jnp.logical_and(o >= 0, o < seq_n)

    cols_of = lambda core: pl.ds(aligned(core, mine), mine)
    w_copy = [
        remote(
            w_qkv.at[j, :, cols_of(other)],
            wfull.at[j, pl.ds(aligned(c, half), half), :],
            send_w.at[j],
            recv_w.at[j],
            cfg=other,
        )
        for j in range(3)
    ]
    w_local = [
        pltpu.make_async_copy(
            w_qkv.at[j, :, cols_of(c)], wfull.at[j, pl.ds(aligned(c, half), half), :], loc.at[j]
        )
        for j in range(3)
    ]
    lat_local = pltpu.make_async_copy(latent, lat.at[z], loc.at[3])
    pos_local = pltpu.make_async_copy(pos_in, pos.at[z], loc.at[4])
    txt_local = pltpu.make_async_copy(text_kv.at[0], txt.at[z], loc.at[5])
    len_local = pltpu.make_async_copy(lens_in, lens.at[c], loc.at[6])
    out_local = pltpu.make_async_copy(w_out, wout, loc.at[7])

    def strip_of(core, s, ten):
        return pl.ds(aligned((core * subs + s) * ten_n + ten, STRIP), STRIP)

    def band_of(core, s):
        return pl.ds(aligned(core * subs + s, band), band)

    def up(d):
        return 0 if d > 0 else 1

    def first_a(s, d):
        at = strip_of(c, s, x)
        return remote(latent.at[at], lat.at[z, at], send_a.at[z, s, up(d)], recv_a.at[z, s], seq=z + d)

    def copy_a(o, s, d):
        at = strip_of(c, s, x)
        return remote(lat.at[o, at], lat.at[o, at], send_a.at[o, s, up(d)], recv_a.at[o, s], seq=z + d)

    def copy_b(o, s, t):
        at = strip_of(c, s, x)
        to = (x + t) % ten_n
        return remote(lat.at[o, at], lat.at[o, at], send_b.at[o, s, t], recv_b.at[o, s, t], tensor=to)

    def arrived_b(o, s, t):
        source = (x + ten_n - t) % ten_n
        at = strip_of(c, s, source)
        return remote(lat.at[o, at], lat.at[o, at], send_b.at[o, s, t], recv_b.at[o, s, t], tensor=source)

    def copy_c(o, s, core):
        at = band_of(core, s)
        return remote(lat.at[o, at], lat.at[o, at], send_c.at[o, s], recv_c.at[o, s], cfg=other)

    def first_p(d):
        return remote(pos_in, pos.at[z], send_p.at[z, up(d)], recv_p.at[z], seq=z + d)

    def copy_p(o, d):
        return remote(pos.at[o], pos.at[o], send_p.at[o, up(d)], recv_p.at[o], seq=z + d)

    def first_t(d):
        return remote(text_kv.at[0], txt.at[z], send_t.at[z, up(d)], recv_t.at[z], seq=z + d)

    def copy_t(o, d):
        return remote(txt.at[o], txt.at[o], send_t.at[o, up(d)], recv_t.at[o], seq=z + d)

    def first_u():
        return remote(
            text_kv.at[0, :, :, cols_of(other)], txo.at[z], send_u.at[z], recv_u.at[z], cfg=other
        )

    def copy_u(o):
        return remote(txt.at[o, :, :, cols_of(other)], txo.at[o], send_u.at[o], recv_u.at[o], cfg=other)

    def copy_l(core):
        return remote(lens_in, lens.at[core], send_l.at[0], recv_l.at[0], cfg=other)

    for j in range(3):
        w_local[j].start()
    lat_local.start()
    pos_local.start()
    txt_local.start()
    len_local.start()
    out_local.start()

    barrier = pltpu.get_barrier_semaphore()
    for d in (1, -1):

        @pl.when(inside(z + d))
        def _():
            pl.semaphore_signal(barrier, inc=1, device_id={"seq": z + d}, device_id_type=MESH)

    pl.semaphore_signal(barrier, inc=1, device_id={"cfg": other}, device_id_type=MESH)
    for t in range(1, ten_n):
        pl.semaphore_signal(
            barrier, inc=1, device_id={"tensor": (x + t) % ten_n}, device_id_type=MESH
        )
    sides = jnp.where(z > 0, 1, 0) + jnp.where(z < seq_n - 1, 1, 0)
    pl.semaphore_wait(barrier, ten_n + sides)

    for d in (1, -1):

        @pl.when(inside(z + d))
        def _():
            first_p(d).start()
            for s in range(subs):
                first_a(s, d).start()

    for j in range(3):
        w_copy[j].start()
    copy_l(c).start()
    first_u().start()
    for d in (1, -1):

        @pl.when(inside(z + d))
        def _():
            first_t(d).start()

    acc[...] = jnp.zeros_like(acc)
    lsum[...] = jnp.zeros_like(lsum)
    lat_local.wait()
    pos_local.wait()

    def pump_a(k, s):
        for d in (1, -1):
            o = z - d * k

            @pl.when(inside(o))
            def _():
                if s == 0:
                    copy_p(o, d).wait_recv()
                copy_a(o, s, d).wait_recv()

                @pl.when(inside(z + d))
                def _():
                    if s == 0:
                        copy_p(o, d).start()
                    copy_a(o, s, d).start()

    def pump_t(k):
        for d in (1, -1):
            o = z - d * k

            @pl.when(inside(o))
            def _():
                copy_t(o, d).wait_recv()

                @pl.when(inside(z + d))
                def _():
                    copy_t(o, d).start()

                copy_u(o).start()

    def start_b(o, s):
        for t in range(1, ten_n):
            copy_b(o, s, t).start()

    def end_b(o, s):
        for t in range(1, ten_n):
            arrived_b(o, s, t).wait_recv()
        copy_c(o, s, c).start()

    slots = 2 * tiles + 3

    def pump(i, slot):
        @pl.when(i + 1 < seq_n)
        def _():
            o = order(i + 1)
            for s in range(subs):
                if slot == min(2 * s, slots - 3):
                    pump_a(i + 1, s)
                    start_b(o, s)
            for s in range(subs):
                if slot == min(2 * s + 1, slots - 2):
                    end_b(o, s)
            if slot == slots - 2:
                pump_t(i + 1)

    def normed_head(value, gain):
        return (
            value * lax.rsqrt(jnp.mean(value * value, axis=-1, keepdims=True) + 1e-06) * gain
        )

    def turned(value):
        total = value * tab[0]
        for k, shift in enumerate(ROT_SHIFTS):
            total = total + pltpu.roll(value, shift, 1) * tab[1 + k]
        return total

    def project(j, t):
        at = pl.ds(t * tile, tile)
        return [
            jnp.dot(mod[b * rows : (b + 1) * rows, :], wfull[j, :, at], preferred_element_type=F32)
            for b in range(2)
        ]

    def head_tile(j, gain_row, dest, t):
        y = project(j, t)
        gain = gains[gain_row : gain_row + 1, :]
        for hh in range(per_tile):
            for b in range(2):
                part_in = y[b][:, hh * HEAD_DIM : (hh + 1) * HEAD_DIM]
                dest[b * heads + t * per_tile + hh] = turned(normed_head(part_in, gain)).astype(BF16)

    def value_tile(t):
        y = [value.astype(BF16) for value in project(2, t)]
        for hh in range(per_tile):
            for b in range(2):
                vbuf[b * heads + t * per_tile + hh] = y[b][:, hh * HEAD_DIM : (hh + 1) * HEAD_DIM]

    def attend(h):
        scores = lax.dot_general(
            qbuf[h], kbuf[h], (((1,), (1,)), ((), ())), preferred_element_type=F32
        )
        expo = jnp.exp(scores * scale)
        folded = expo[:, :HEAD_DIM]
        for k in range(1, rows // HEAD_DIM):
            folded = folded + expo[:, k * HEAD_DIM : (k + 1) * HEAD_DIM]
        lsum[h] += folded
        acc[h] += jnp.dot(expo.astype(BF16), vbuf[h], preferred_element_type=F32)

    @pl.loop(0, seq_n)
    def _(i):
        o = order(i)

        @pl.when(i > 0)
        def _():
            for s in range(subs):
                copy_c(o, s, other).wait_recv()

        place = lax.dot_general(
            pos[o], pick[...], (((0,), (0,)), ((), ())), preferred_element_type=F32
        )
        angle = place * rot[0:1, :]
        sine = jnp.sin(angle)
        tab[0] = jnp.cos(angle)
        for k in range(len(ROT_SHIFTS)):
            tab[1 + k] = sine * rot[1 + k : 2 + k, :]

        @pl.loop(0, rows // STRIP, unroll=U_MOD)
        def _(r):
            at = pl.ds(pl.multiple_of(r * STRIP, STRIP), STRIP)
            value = lat[o, at, :].astype(F32)
            center = value - jnp.mean(value, axis=-1, keepdims=True)
            normed = center * lax.rsqrt(jnp.mean(center * center, axis=-1, keepdims=True) + 1e-06)
            for b in range(2):
                mod[pl.ds(pl.multiple_of(b * rows + r * STRIP, STRIP), STRIP), :] = (
                    normed * (1.0 + modulation[1, b : b + 1, :]) + modulation[0, b : b + 1, :]
                ).astype(BF16)

        @pl.when(i == 0)
        def _():
            w_local[0].wait()
            w_copy[0].wait_recv()
            for t in range(tiles):
                head_tile(0, 0, qbuf, t)
            w_local[1].wait()
            w_copy[1].wait_recv()

        for t in range(tiles):
            head_tile(1, 1, kbuf, t)
            pump(i, t)

        @pl.when(i == 0)
        def _():
            w_local[2].wait()
            w_copy[2].wait_recv()

        for t in range(tiles):
            value_tile(t)
            pump(i, tiles + t)

        group = (2 * heads + 2) // 3
        for g in range(3):

            @pl.loop(g * group, min((g + 1) * group, 2 * heads), unroll=True)
            def _(h):
                attend(h)

            pump(i, 2 * tiles + g)

    txt_local.wait()
    len_local.wait()
    copy_l(other).wait_recv()

    @pl.loop(0, seq_n)
    def _(o):
        copy_u(o).wait_recv()

    text_rows = txt.shape[2]
    count = seq_n * text_rows

    def copy_o(core, branch):
        return remote(
            attf.at[core, branch], attf.at[core, branch], send_o.at[branch], recv_o.at[branch], cfg=other
        )

    for own in range(2):
        branch = c if own == 0 else other
        source = txt if own == 0 else txo
        base = aligned(c, mine) if own == 0 else 0
        valid = lax.broadcasted_iota(jnp.int32, (1, count), 1).astype(F32) < lens[branch, 0:1, :]

        @pl.loop(0, heads, unroll=U_TEXT)
        def _(h):
            at = pl.ds(pl.multiple_of(h * HEAD_DIM, HEAD_DIM), HEAD_DIM)
            src = pl.ds(pl.multiple_of(base + h * HEAD_DIM, HEAD_DIM), HEAD_DIM)
            raw = source[:, 0, :, src].reshape(count, HEAD_DIM).astype(F32)
            keys = normed_head(raw, gains[1:2, :]).astype(BF16)
            values = source[:, 1, :, src].reshape(count, HEAD_DIM)
            n = branch * heads + h
            scores = lax.dot_general(
                qbuf[n], keys, (((1,), (1,)), ((), ())), preferred_element_type=F32
            )
            expo = jnp.where(valid, jnp.exp(scores * scale), 0.0)
            total = jnp.sum(lsum[n], axis=-1, keepdims=True) + jnp.sum(
                expo, axis=-1, keepdims=True
            )
            mixed = acc[n] + jnp.dot(expo.astype(BF16), values, preferred_element_type=F32)
            attf[c, branch, :, at] = (mixed / total).astype(BF16)

        copy_o(c, branch).start()

    out_local.wait()
    copy_o(other, other).wait_recv()
    copy_o(other, c).wait_recv()

    out_tile = 256 if out_cols % 256 == 0 else 128
    out_tiles = out_cols // out_tile

    def copy_r(t, k):
        return remote(
            part.at[t, k], got.at[t, k], send_r.at[t, k], recv_r.at[t, k], tensor=(x + t) % ten_n
        )

    def out_block(t, k):
        to = (x + t) % ten_n
        here = pl.ds(pl.multiple_of(to * out_rows, out_rows), out_rows)
        at = pl.ds(pl.multiple_of(k * out_tile, out_tile), out_tile)
        total = None
        strength = guide[0:1, 0:1]
        at_gate = pl.ds(pl.multiple_of(c * out_cols + k * out_tile, out_tile), out_tile)
        gates = (
            strength * modulation[2, 0:1, at_gate],
            (1.0 - strength) * modulation[2, 1:2, at_gate],
        )
        for b in range(2):
            y = jnp.dot(attf[0, b, here, :], wout[0:mine, at], preferred_element_type=F32)
            y = y + jnp.dot(
                attf[1, b, here, :], wout[mine : 2 * mine, at], preferred_element_type=F32
            )
            y = y * gates[b]
            total = y if total is None else total + y
        return total

    for t in range(1, ten_n):

        @pl.loop(0, out_tiles)
        def _(k):
            part[t, k] = out_block(t, k).astype(BF16)
            copy_r(t, k).start()

    @pl.loop(0, out_tiles)
    def _(k):
        part[0, k] = out_block(0, k).astype(BF16)

    for k in range(out_tiles):
        total = part[0, k].astype(F32)
        for t in range(1, ten_n):
            copy_r(t, k).wait_recv()
            total = total + got[t, k].astype(F32)
        out[:, k * out_tile : (k + 1) * out_tile] = total.astype(BF16)

    for j in range(3):
        w_copy[j].wait_send()
    copy_l(c).wait_send()
    for b in range(2):
        copy_o(c, b).wait_send()
    for t in range(1, ten_n):
        for k in range(out_tiles):
            copy_r(t, k).wait_send()

    @pl.loop(0, seq_n)
    def _(o):
        copy_u(o).wait_send()

        @pl.when(o != z)
        def _():
            for s in range(subs):
                for t in range(1, ten_n):
                    copy_b(o, s, t).wait_send()
                copy_c(o, s, c).wait_send()

        for d in (1, -1):
            ahead = jnp.logical_or(o == z, d * (z - o) > 0)

            @pl.when(jnp.logical_and(ahead, inside(z + d)))
            def _():
                copy_p(o, d).wait_send()
                copy_t(o, d).wait_send()
                for s in range(subs):
                    copy_a(o, s, d).wait_send()


def local(
    seq_n, ten_n, latent, positions, text_kv, text_len, modulation, w_qkv, norm_gains, w_out, guidance
):
    rows, width = latent.shape
    mine = w_qkv.shape[2] // 2
    heads = mine // HEAD_DIM
    text_dev = text_kv.shape[2]
    out_rows = rows // ten_n
    out_cols = w_out.shape[1]
    out_tile = 256 if out_cols % 256 == 0 else 128
    out_tiles = out_cols // out_tile
    subs = rows // (2 * ten_n * STRIP)
    pos_in = jnp.pad(positions.astype(BF16), ((0, 13), (0, 0)))
    lens = jnp.broadcast_to(text_len.astype(F32)[None, :], (8, seq_n * text_dev))
    any_space = pl.BlockSpec(memory_space=pl.ANY)
    vmem = pl.BlockSpec(memory_space=pltpu.VMEM)
    dma = pltpu.SemaphoreType.DMA
    return pl.pallas_call(
        functools.partial(kernel, seq_n, ten_n),
        out_shape=jax.ShapeDtypeStruct((out_rows, out_cols), BF16),
        in_specs=[
            any_space,
            any_space,
            any_space,
            any_space,
            vmem,
            any_space,
            vmem,
            any_space,
            vmem,
            vmem,
            vmem,
        ],
        out_specs=vmem,
        scratch_shapes=[
            pltpu.VMEM((seq_n, rows, width), BF16),
            pltpu.VMEM((seq_n, 16, rows), BF16),
            pltpu.VMEM((seq_n, 2, text_dev, 2 * mine), BF16),
            pltpu.VMEM((seq_n, 2, text_dev, mine), BF16),
            pltpu.VMEM((2, 8, seq_n * text_dev), F32),
            pltpu.VMEM((3, width, mine), BF16),
            pltpu.VMEM(w_out.shape, BF16),
            pltpu.VMEM((2 * rows, width), BF16),
            pltpu.VMEM((1 + len(ROT_SHIFTS), rows, HEAD_DIM), F32),
            pltpu.VMEM((2 * heads, rows, HEAD_DIM), BF16),
            pltpu.VMEM((2 * heads, rows, HEAD_DIM), BF16),
            pltpu.VMEM((2 * heads, rows, HEAD_DIM), BF16),
            pltpu.VMEM((2 * heads, rows, HEAD_DIM), F32),
            pltpu.VMEM((2 * heads, rows, HEAD_DIM), F32),
            pltpu.VMEM((2, 2, rows, mine), BF16),
            pltpu.VMEM((ten_n, out_tiles, out_rows, out_tile), BF16),
            pltpu.VMEM((ten_n, out_tiles, out_rows, out_tile), BF16),
            dma((seq_n, subs, 2)),
            dma((seq_n, subs)),
            dma((seq_n, subs, ten_n)),
            dma((seq_n, subs, ten_n)),
            dma((seq_n, subs)),
            dma((seq_n, subs)),
            dma((seq_n, 2)),
            dma((seq_n,)),
            dma((seq_n, 2)),
            dma((seq_n,)),
            dma((seq_n,)),
            dma((seq_n,)),
            dma((3,)),
            dma((3,)),
            dma((1,)),
            dma((1,)),
            dma((2,)),
            dma((2,)),
            dma((ten_n, out_tiles)),
            dma((ten_n, out_tiles)),
            dma((8,)),
        ],
        compiler_params=pltpu.CompilerParams(
            collective_id=0, has_side_effects=True, vmem_limit_bytes=64 * 1024 * 1024 - 65536
        ),
    )(
        latent,
        pos_in,
        text_kv,
        lens,
        modulation,
        w_qkv,
        norm_gains,
        w_out,
        guidance.reshape(1, 1),
        jnp.asarray(ROT_ROWS),
        jnp.asarray(ROT_PICK, BF16),
    )


def solution(mesh):
    placed = (
        P(("groups", "seq"), None),
        P(None, ("groups", "seq")),
        P("cfg", None, ("groups", "seq"), "tensor"),
        P(("groups", "cfg")),
        P(None, "groups", None),
        P(None, "cfg", "tensor"),
        P(),
        P("tensor", "cfg"),
        P("groups"),
    )
    return jax.shard_map(
        functools.partial(local, mesh.shape["seq"], mesh.shape["tensor"]),
        mesh=mesh,
        in_specs=placed,
        out_specs=P(("groups", "seq", "tensor"), "cfg"),
        check_vma=False,
    )
```

time: 105 us -> 117 us (1.11)
  Pallas kernels: 99.7 us -> 111 us
    pallas_call x1, Pallas kernels: 99.7 us -> 111 us  [local(): pl.pallas_call(functools.partial(kernel, seq_n, ten_n), out_shape=jax.Sha...]
where the time goes in v1:
time: 117 us; the launch traced here: 116 us
  Pallas kernels  111 us (95%)
  local copies, waits for them, and re-layouts  2.95 us (3%)
  between operations  1.31 us (1%)
    pallas_call x1, Pallas kernels, local(): pl.pallas_call(functools.partial(kernel, seq_n, ten_n), out_shape=jax.Sha...  111 us

profile of v1, /device:TPU:0, one launch (start us, length us, event | category | flops | bytes accessed | tf_op | source)
XLA Modules:
  0.0 116.4 jit_solution(16252079022458379220)
XLA Ops:
  1.3 0.7 convert_element_type.8
  2.0 0.6 broadcast_in_dim.9.lens_in
  2.6 0.6 pad.4.pos_in
  3.2 111.4 %shard_map.109 = bf16[128,1536]{1,0:T(8,128)(2,1)} custom-call(bf16[256,3072]{1,0:T(8,128)(2,1)} %latent.1, bf16[16,256]{1,0:T(8,128)(2,1)} %pad.4.pos_in, bf16[1,2,16,1536]{3,2,1,0:T(8,128)(2,1)} %text_kv.1, f32[8,64]{1,0:T(8,128)} %broadcast_in_dim.9.lens_in, f32[3,2,3072]{2,1,0:T(2,128)} %modulation.1, bf16[3,1536,1536]{2,1,0:T(8,128)(2,1)} %w_qkv.1, ...), custom_call_target="tpu_custom_call" | custom-call | tf_op jit(solution)/shard_map/pallas_call | solution.py:564
  114.6 1.8 %copy.15 = bf16[128,1536]{1,0:T(8,128)(2,1)} copy(bf16[128,1536]{1,0:T(8,128)(2,1)} %shard_map.109) | data formatting | bytes 786432

commit v2 on v1

--- a/solution.py
+++ b/solution.py
@@ -1,4 +1,5 @@
 import functools
+import math
 
 import jax
 import jax.numpy as jnp
@@ -10,40 +11,44 @@
 
 HEAD_DIM = 128
 MESH = pl.DeviceIdType.MESH
-U_TILE = True
 U_MOD = 8
-U_ATT = 4
-U_TEXT = 2
 F32 = jnp.float32
 BF16 = jnp.bfloat16
 
 
 def rotary_rows(head_size):
     rows = np.zeros((8, head_size), np.float32)
+    swap = np.zeros((head_size, head_size), np.float32)
     axes = np.zeros((head_size,), np.int32)
     blocks = (head_size // 8, 7 * head_size // 16, 7 * head_size // 16)
-    halves = []
     offset = 0
     for axis_id, width in enumerate(blocks):
         half = width // 2
-        if half not in halves:
-            halves.append(half)
-        which = halves.index(half)
-        freq = (256.0 ** (-np.arange(half, dtype=np.float64) / half)).astype(np.float32)
-        rows[0, offset : offset + half] = freq
-        rows[0, offset + half : offset + width] = freq
-        rows[1 + 2 * which, offset : offset + half] = -1.0
-        rows[2 + 2 * which, offset + half : offset + width] = 1.0
+        turns = 256.0 ** (-np.arange(half, dtype=np.float64) / half) / (2 * np.pi)
+        rows[0, offset : offset + half] = turns
+        rows[0, offset + half : offset + width] = turns
+        for k in range(half):
+            swap[offset + half + k, offset + k] = -1.0
+            swap[offset + k, offset + half + k] = 1.0
         axes[offset : offset + width] = axis_id
         offset += width
-    shifts = []
-    for half in halves:
-        shifts += [head_size - half, half]
-    return rows, axes, tuple(shifts)
-
-
-ROT_ROWS, ROT_AXES, ROT_SHIFTS = rotary_rows(HEAD_DIM)
+    return rows, axes, swap
+
+
+ROT_ROWS, ROT_AXES, ROT_SWAP = rotary_rows(HEAD_DIM)
 ROT_PICK = (np.arange(16)[:, None] == ROT_AXES[None, :]).astype(np.float32)
+SIDE = np.kron(np.eye(2), np.ones((HEAD_DIM, HEAD_DIM)))
+MIX = np.stack([np.kron(np.eye(2), ROT_SWAP), SIDE / HEAD_DIM]).astype(np.float32)
+SIN = tuple((-1.0) ** k / math.factorial(2 * k + 1) for k in range(6))
+COS = tuple((-1.0) ** k / math.factorial(2 * k) for k in range(6))
+LOG2E = 1.4426950408889634
+
+
+def horner(terms, value):
+    total = terms[-1]
+    for term in terms[-2::-1]:
+        total = total * value + term
+    return total
 
 
 STRIP = 16
@@ -63,6 +68,7 @@
     guide,
     rot,
     pick,
+    mix,
     out,
     lat,
     pos,
@@ -116,7 +122,7 @@
     subs = half_rows // band
     out_rows = rows // ten_n
     out_cols = w_out.shape[1]
-    scale = HEAD_DIM ** (-0.5)
+    scale = HEAD_DIM ** (-0.5) * LOG2E
     tile = 256 if mine % 256 == 0 else 128
     per_tile = tile // HEAD_DIM
     tiles = mine // tile
@@ -172,10 +178,6 @@
     def up(d):
         return 0 if d > 0 else 1
 
-    def first_a(s, d):
-        at = strip_of(c, s, x)
-        return remote(latent.at[at], lat.at[z, at], send_a.at[z, s, up(d)], recv_a.at[z, s], seq=z + d)
-
     def copy_a(o, s, d):
         at = strip_of(c, s, x)
         return remote(lat.at[o, at], lat.at[o, at], send_a.at[o, s, up(d)], recv_a.at[o, s], seq=z + d)
@@ -237,6 +239,17 @@
         pl.semaphore_signal(
             barrier, inc=1, device_id={"tensor": (x + t) % ten_n}, device_id_type=MESH
         )
+
+    def normalize(at):
+        value = lat[z, at, :].astype(F32)
+        center = value - jnp.mean(value, axis=-1, keepdims=True)
+        normed = center * lax.rsqrt(jnp.mean(center * center, axis=-1, keepdims=True) + 1e-06)
+        lat[z, at, :] = normed.astype(BF16)
+
+    lat_local.wait()
+    for s in range(subs):
+        normalize(strip_of(c, s, x))
+
     sides = jnp.where(z > 0, 1, 0) + jnp.where(z < seq_n - 1, 1, 0)
     pl.semaphore_wait(barrier, ten_n + sides)
 
@@ -246,7 +259,7 @@
         def _():
             first_p(d).start()
             for s in range(subs):
-                first_a(s, d).start()
+                copy_a(z, s, d).start()
 
     for j in range(3):
         w_copy[j].start()
@@ -258,9 +271,14 @@
         def _():
             first_t(d).start()
 
-    acc[...] = jnp.zeros_like(acc)
-    lsum[...] = jnp.zeros_like(lsum)
-    lat_local.wait()
+    for t in range(1, ten_n):
+        for s in range(subs):
+            normalize(strip_of(c, s, (x + t) % ten_n))
+
+    @pl.loop(0, half_rows // STRIP, unroll=4)
+    def _(r):
+        normalize(pl.ds(aligned(other * (half_rows // STRIP) + r, STRIP), STRIP))
+
     pos_local.wait()
 
     def pump_a(k, s):
@@ -302,124 +320,167 @@
             arrived_b(o, s, t).wait_recv()
         copy_c(o, s, c).start()
 
-    slots = 2 * tiles + 3
-
-    def pump(i, slot):
-        @pl.when(i + 1 < seq_n)
-        def _():
-            o = order(i + 1)
-            for s in range(subs):
-                if slot == min(2 * s, slots - 3):
-                    pump_a(i + 1, s)
-                    start_b(o, s)
-            for s in range(subs):
-                if slot == min(2 * s + 1, slots - 2):
-                    end_b(o, s)
-            if slot == slots - 2:
-                pump_t(i + 1)
-
-    def normed_head(value, gain):
-        return (
-            value * lax.rsqrt(jnp.mean(value * value, axis=-1, keepdims=True) + 1e-06) * gain
-        )
-
-    def turned(value):
-        total = value * tab[0]
-        for k, shift in enumerate(ROT_SHIFTS):
-            total = total + pltpu.roll(value, shift, 1) * tab[1 + k]
-        return total
-
-    def project(j, t):
-        at = pl.ds(t * tile, tile)
-        return [
-            jnp.dot(mod[b * rows : (b + 1) * rows, :], wfull[j, :, at], preferred_element_type=F32)
-            for b in range(2)
-        ]
-
-    def head_tile(j, gain_row, dest, t):
-        y = project(j, t)
-        gain = gains[gain_row : gain_row + 1, :]
-        for hh in range(per_tile):
-            for b in range(2):
-                part_in = y[b][:, hh * HEAD_DIM : (hh + 1) * HEAD_DIM]
-                dest[b * heads + t * per_tile + hh] = turned(normed_head(part_in, gain)).astype(BF16)
-
-    def value_tile(t):
-        y = [value.astype(BF16) for value in project(2, t)]
-        for hh in range(per_tile):
-            for b in range(2):
-                vbuf[b * heads + t * per_tile + hh] = y[b][:, hh * HEAD_DIM : (hh + 1) * HEAD_DIM]
-
-    def attend(h):
-        scores = lax.dot_general(
-            qbuf[h], kbuf[h], (((1,), (1,)), ((), ())), preferred_element_type=F32
-        )
-        expo = jnp.exp(scores * scale)
-        folded = expo[:, :HEAD_DIM]
-        for k in range(1, rows // HEAD_DIM):
-            folded = folded + expo[:, k * HEAD_DIM : (k + 1) * HEAD_DIM]
-        lsum[h] += folded
-        acc[h] += jnp.dot(expo.astype(BF16), vbuf[h], preferred_element_type=F32)
-
-    @pl.loop(0, seq_n)
-    def _(i):
-        o = order(i)
-
-        @pl.when(i > 0)
+    def front(k, p):
+        @pl.when(k < seq_n)
         def _():
             for s in range(subs):
-                copy_c(o, s, other).wait_recv()
-
+                if s * 4 // subs == p:
+                    pump_a(k, s)
+                    start_b(order(k), s)
+
+    def back(k, p):
+        @pl.when(k < seq_n)
+        def _():
+            for s in range(subs):
+                if s * 4 // subs == p:
+                    end_b(order(k), s)
+
+    slots = 2 * tiles + 2
+
+    def pump(i, slot):
+        if slot == 0:
+            front(i + 1, 2)
+        if slot == 1:
+            front(i + 1, 3)
+        if slot == tiles:
+            back(i + 1, 0)
+        if slot == 2 * tiles - 1:
+            back(i + 1, 1)
+
+            @pl.when(i + 1 < seq_n)
+            def _():
+                pump_t(i + 1)
+
+        if slot == 2 * tiles:
+            back(i + 1, 2)
+            front(i + 2, 0)
+        if slot == slots - 1:
+            back(i + 1, 3)
+            front(i + 2, 1)
+
+    def project(j, t, b):
+        at = pl.ds(t * tile, tile)
+        return jnp.dot(
+            mod[b * rows : (b + 1) * rows, :], wfull[j, :, at], preferred_element_type=F32
+        )
+
+    def finish(j, t, b, y):
+        if j == 2:
+            y = y.astype(BF16)
+            for hh in range(per_tile):
+                vbuf[b * heads + t * per_tile + hh] = y[:, hh * HEAD_DIM : (hh + 1) * HEAD_DIM]
+            return
+        swapped = jnp.dot(y.astype(BF16), mix[0, :tile, :tile], preferred_element_type=F32)
+        square = jnp.dot((y * y).astype(BF16), mix[1, :tile, :tile], preferred_element_type=F32)
+        inverse = lax.rsqrt(square + 1e-06)
+        dest = kbuf if j == 1 else qbuf
+        for hh in range(per_tile):
+            at = slice(hh * HEAD_DIM, (hh + 1) * HEAD_DIM)
+            turned = y[:, at] * tab[2 * j] + swapped[:, at] * tab[2 * j + 1]
+            dest[b * heads + t * per_tile + hh] = (turned * inverse[:, at]).astype(BF16)
+
+    def attend(span, first):
+        ahead = {}
+        for n in range(len(span) + 2):
+            if n < len(span):
+                h = span[n]
+                ahead[n] = lax.dot_general(
+                    qbuf[h], kbuf[h], (((1,), (1,)), ((), ())), preferred_element_type=F32
+                )
+            if n < 2:
+                continue
+            h = span[n - 2]
+            expo = jnp.exp2(ahead.pop(n - 2))
+            folded = expo[:, :HEAD_DIM]
+            for k in range(1, rows // HEAD_DIM):
+                folded = folded + expo[:, k * HEAD_DIM : (k + 1) * HEAD_DIM]
+            mixed = jnp.dot(expo.astype(BF16), vbuf[h], preferred_element_type=F32)
+            if first:
+                lsum[h] = folded
+                acc[h] = mixed
+            else:
+                lsum[h] += folded
+                acc[h] += mixed
+
+    def tables(o, first):
         place = lax.dot_general(
             pos[o], pick[...], (((0,), (0,)), ((), ())), preferred_element_type=F32
         )
-        angle = place * rot[0:1, :]
-        sine = jnp.sin(angle)
-        tab[0] = jnp.cos(angle)
-        for k in range(len(ROT_SHIFTS)):
-            tab[1 + k] = sine * rot[1 + k : 2 + k, :]
-
-        @pl.loop(0, rows // STRIP, unroll=U_MOD)
+        turns = place * rot[0:1, :]
+        angle = (turns - jnp.floor(turns + 0.5)) * math.pi
+        square = angle * angle
+        low = angle * horner(SIN, square)
+        cosine = 1.0 - 2.0 * low * low
+        sine = 2.0 * low * horner(COS, square)
+        for j in range(0 if first else 1, 2):
+            strength = scale if j == 0 else 1.0
+            tab[2 * j] = cosine * (gain_rows[j][0:1] * strength)
+            tab[2 * j + 1] = sine * (gain_rows[j][1:2] * strength)
+
+    swap_abs = jnp.abs(mix[0, :HEAD_DIM, :HEAD_DIM].astype(F32))
+    gain_rows = []
+    for j in range(2):
+        own = gains[j : j + 1, :]
+        column = jnp.sum(
+            jnp.where(
+                lax.broadcasted_iota(jnp.int32, (HEAD_DIM, HEAD_DIM), 0)
+                == lax.broadcasted_iota(jnp.int32, (HEAD_DIM, HEAD_DIM), 1),
+                own,
+                0.0,
+            ),
+            axis=1,
+            keepdims=True,
+        )
+        gain_rows.append(jnp.concatenate([own, jnp.sum(swap_abs * column, axis=0, keepdims=True)]))
+
+    def modulate(o, core):
+        @pl.loop(0, half_rows // STRIP, unroll=U_MOD)
         def _(r):
-            at = pl.ds(pl.multiple_of(r * STRIP, STRIP), STRIP)
-            value = lat[o, at, :].astype(F32)
-            center = value - jnp.mean(value, axis=-1, keepdims=True)
-            normed = center * lax.rsqrt(jnp.mean(center * center, axis=-1, keepdims=True) + 1e-06)
+            start = aligned(core * (half_rows // STRIP) + r, STRIP)
+            normed = lat[o, pl.ds(start, STRIP), :].astype(F32)
             for b in range(2):
-                mod[pl.ds(pl.multiple_of(b * rows + r * STRIP, STRIP), STRIP), :] = (
+                mod[pl.ds(pl.multiple_of(b * rows + start, STRIP), STRIP), :] = (
                     normed * (1.0 + modulation[1, b : b + 1, :]) + modulation[0, b : b + 1, :]
                 ).astype(BF16)
 
-        @pl.when(i == 0)
-        def _():
-            w_local[0].wait()
-            w_copy[0].wait_recv()
+    def step(i, first):
+        o = order(i)
+        tables(o, first)
+        modulate(o, c)
+        if not first:
+            for s in range(subs):
+                copy_c(o, s, other).wait_recv()
+        modulate(o, other)
+
+        pending = None
+        for j in range(0 if first else 1, 3):
+            if first:
+                w_local[j].wait()
+                w_copy[j].wait_recv()
             for t in range(tiles):
-                head_tile(0, 0, qbuf, t)
-            w_local[1].wait()
-            w_copy[1].wait_recv()
-
-        for t in range(tiles):
-            head_tile(1, 1, kbuf, t)
-            pump(i, t)
-
-        @pl.when(i == 0)
-        def _():
-            w_local[2].wait()
-            w_copy[2].wait_recv()
-
-        for t in range(tiles):
-            value_tile(t)
-            pump(i, tiles + t)
-
-        group = (2 * heads + 2) // 3
-        for g in range(3):
-
-            @pl.loop(g * group, min((g + 1) * group, 2 * heads), unroll=True)
-            def _(h):
-                attend(h)
-
+                for b in range(2):
+                    y = project(j, t, b)
+                    if pending is not None:
+                        finish(*pending)
+                    pending = (j, t, b, y)
+                if j > 0:
+                    pump(i, (j - 1) * tiles + t)
+                    continue
+                if t == max(tiles - 2, 0):
+                    front(1, 0)
+                if t == tiles - 1:
+                    front(1, 1)
+        finish(*pending)
+        group = heads
+        for g in range(2):
+            attend(list(range(g * group, (g + 1) * group)), first)
             pump(i, 2 * tiles + g)
+
+    step(0, True)
+
+    @pl.loop(1, seq_n)
+    def _(i):
+        step(i, False)
 
     txt_local.wait()
     len_local.wait()
@@ -433,8 +494,9 @@
     count = seq_n * text_rows
 
     def copy_o(core, branch):
+        at = pl.ds(aligned(branch, out_rows), out_rows)
         return remote(
-            attf.at[core, branch], attf.at[core, branch], send_o.at[branch], recv_o.at[branch], cfg=other
+            attf.at[core, :, at], attf.at[core, :, at], send_o.at[branch], recv_o.at[branch], cfg=other
         )
 
     for own in range(2):
@@ -442,24 +504,32 @@
         source = txt if own == 0 else txo
         base = aligned(c, mine) if own == 0 else 0
         valid = lax.broadcasted_iota(jnp.int32, (1, count), 1).astype(F32) < lens[branch, 0:1, :]
-
-        @pl.loop(0, heads, unroll=U_TEXT)
-        def _(h):
-            at = pl.ds(pl.multiple_of(h * HEAD_DIM, HEAD_DIM), HEAD_DIM)
+        ahead = {}
+        for step_n in range(heads + 2):
+            if step_n < heads:
+                src = pl.ds(pl.multiple_of(base + step_n * HEAD_DIM, HEAD_DIM), HEAD_DIM)
+                raw = source[:, 0, :, src].reshape(count, HEAD_DIM).astype(F32)
+                inverse = lax.rsqrt(jnp.mean(raw * raw, axis=-1, keepdims=True) + 1e-06)
+                keys = (raw * inverse * gains[1:2, :]).astype(BF16)
+                ahead[step_n] = lax.dot_general(
+                    qbuf[branch * heads + step_n], keys, (((1,), (1,)), ((), ())), preferred_element_type=F32
+                )
+            if step_n < 2:
+                continue
+            h = step_n - 2
+            n = branch * heads + h
             src = pl.ds(pl.multiple_of(base + h * HEAD_DIM, HEAD_DIM), HEAD_DIM)
-            raw = source[:, 0, :, src].reshape(count, HEAD_DIM).astype(F32)
-            keys = normed_head(raw, gains[1:2, :]).astype(BF16)
             values = source[:, 1, :, src].reshape(count, HEAD_DIM)
-            n = branch * heads + h
-            scores = lax.dot_general(
-                qbuf[n], keys, (((1,), (1,)), ((), ())), preferred_element_type=F32
-            )
-            expo = jnp.where(valid, jnp.exp(scores * scale), 0.0)
+            expo = jnp.where(valid, jnp.exp2(ahead.pop(h)), 0.0)
             total = jnp.sum(lsum[n], axis=-1, keepdims=True) + jnp.sum(
                 expo, axis=-1, keepdims=True
             )
             mixed = acc[n] + jnp.dot(expo.astype(BF16), values, preferred_element_type=F32)
-            attf[c, branch, :, at] = (mixed / total).astype(BF16)
+            result = (mixed * (1.0 / total)).astype(BF16)
+            for t in range(ten_n):
+                attf[c, t, pl.ds(aligned(branch, out_rows), out_rows), h * HEAD_DIM : (h + 1) * HEAD_DIM] = (
+                    result[t * out_rows : (t + 1) * out_rows]
+                )
 
         copy_o(c, branch).start()
 
@@ -475,35 +545,25 @@
             part.at[t, k], got.at[t, k], send_r.at[t, k], recv_r.at[t, k], tensor=(x + t) % ten_n
         )
 
+    strength = guide[0:1, 0:1]
+
     def out_block(t, k):
         to = (x + t) % ten_n
-        here = pl.ds(pl.multiple_of(to * out_rows, out_rows), out_rows)
-        at = pl.ds(pl.multiple_of(k * out_tile, out_tile), out_tile)
-        total = None
-        strength = guide[0:1, 0:1]
+        at = pl.ds(k * out_tile, out_tile)
+        y = jnp.dot(attf[0, to], wout[0:mine, at], preferred_element_type=F32)
+        y = y + jnp.dot(attf[1, to], wout[mine : 2 * mine, at], preferred_element_type=F32)
         at_gate = pl.ds(pl.multiple_of(c * out_cols + k * out_tile, out_tile), out_tile)
-        gates = (
-            strength * modulation[2, 0:1, at_gate],
-            (1.0 - strength) * modulation[2, 1:2, at_gate],
-        )
-        for b in range(2):
-            y = jnp.dot(attf[0, b, here, :], wout[0:mine, at], preferred_element_type=F32)
-            y = y + jnp.dot(
-                attf[1, b, here, :], wout[mine : 2 * mine, at], preferred_element_type=F32
-            )
-            y = y * gates[b]
-            total = y if total is None else total + y
-        return total
+        return (
+            y[:out_rows] * (strength * modulation[2, 0:1, at_gate])
+            + y[out_rows:] * ((1.0 - strength) * modulation[2, 1:2, at_gate])
+        )
 
     for t in range(1, ten_n):
-
-        @pl.loop(0, out_tiles)
-        def _(k):
+        for k in range(out_tiles):
             part[t, k] = out_block(t, k).astype(BF16)
             copy_r(t, k).start()
 
-    @pl.loop(0, out_tiles)
-    def _(k):
+    for k in range(out_tiles):
         part[0, k] = out_block(0, k).astype(BF16)
 
     for k in range(out_tiles):
@@ -576,6 +636,7 @@
             vmem,
             vmem,
             vmem,
+            vmem,
         ],
         out_specs=vmem,
         scratch_shapes=[
@@ -587,13 +648,13 @@
             pltpu.VMEM((3, width, mine), BF16),
             pltpu.VMEM(w_out.shape, BF16),
             pltpu.VMEM((2 * rows, width), BF16),
-            pltpu.VMEM((1 + len(ROT_SHIFTS), rows, HEAD_DIM), F32),
+            pltpu.VMEM((4, rows, HEAD_DIM), F32),
             pltpu.VMEM((2 * heads, rows, HEAD_DIM), BF16),
             pltpu.VMEM((2 * heads, rows, HEAD_DIM), BF16),
             pltpu.VMEM((2 * heads, rows, HEAD_DIM), BF16),
             pltpu.VMEM((2 * heads, rows, HEAD_DIM), F32),
             pltpu.VMEM((2 * heads, rows, HEAD_DIM), F32),
-            pltpu.VMEM((2, 2, rows, mine), BF16),
+            pltpu.VMEM((2, ten_n, 2 * out_rows, mine), BF16),
             pltpu.VMEM((ten_n, out_tiles, out_rows, out_tile), BF16),
             pltpu.VMEM((ten_n, out_tiles, out_rows, out_tile), BF16),
             dma((seq_n, subs, 2)),
@@ -633,6 +694,7 @@
         guidance.reshape(1, 1),
         jnp.asarray(ROT_ROWS),
         jnp.asarray(ROT_PICK, BF16),
+        jnp.asarray(MIX, BF16),
     )
 
 

time: 117 us -> 76.6 us (0.65)
  Pallas kernels: 111 us -> 71.4 us
    pallas_call x1, Pallas kernels: 111 us -> 71.4 us  [local(): pl.pallas_call(functools.partial(kernel, seq_n, ten_n), out_shape=jax.Sha...]
where the time goes in v2:
time: 76.6 us; the launch traced here: 76.4 us
  Pallas kernels  71.4 us (93%)
  local copies, waits for them, and re-layouts  2.95 us (4%)
  between operations  1.31 us (2%)
    pallas_call x1, Pallas kernels, local(): pl.pallas_call(functools.partial(kernel, seq_n, ten_n), out_shape=jax.Sha...  71.4 us
    unnamed x1, local copies, waits for them, and re-layouts  1.77 us

profile of v2, /device:TPU:0, one launch (start us, length us, event | category | flops | bytes accessed | tf_op | source)
XLA Modules:
  0.0 76.4 jit_solution(10771355314009969762)
XLA Ops:
  1.3 0.7 convert_element_type.8
  2.0 0.6 broadcast_in_dim.9.lens_in
  2.6 0.6 pad.4.pos_in
  3.2 71.4 %shard_map.118 = bf16[128,1536]{1,0:T(8,128)(2,1)} custom-call(bf16[256,3072]{1,0:T(8,128)(2,1)} %latent.1, bf16[16,256]{1,0:T(8,128)(2,1)} %pad.4.pos_in, bf16[1,2,16,1536]{3,2,1,0:T(8,128)(2,1)} %text_kv.1, f32[8,64]{1,0:T(8,128)} %broadcast_in_dim.9.lens_in, f32[3,2,3072]{2,1,0:T(2,128)} %modulation.1, bf16[3,1536,1536]{2,1,0:T(8,128)(2,1)} %w_qkv.1, ...), custom_call_target="tpu_custom_call" | custom-call | tf_op jit(solution)/shard_map/pallas_call | solution.py:624
  74.6 1.8 %copy.16 = bf16[128,1536]{1,0:T(8,128)(2,1)} copy(bf16[128,1536]{1,0:T(8,128)(2,1)} %shard_map.118) | data formatting | bytes 786432

commit v3 on v2

--- a/solution.py
+++ b/solution.py
@@ -265,11 +265,6 @@
         w_copy[j].start()
     copy_l(c).start()
     first_u().start()
-    for d in (1, -1):
-
-        @pl.when(inside(z + d))
-        def _():
-            first_t(d).start()
 
     for t in range(1, ten_n):
         for s in range(subs):
@@ -337,26 +332,43 @@
 
     slots = 2 * tiles + 2
 
+    def text_front(i, slot):
+        last = seq_n - 1
+        if slot == tiles:
+            for d in (1, -1):
+
+                @pl.when(jnp.logical_and(i == 1, inside(z + d)))
+                def _():
+                    first_t(d).start()
+
+        if slot == 1 and last > 1:
+
+            @pl.when(i == last)
+            def _():
+                pump_t(last - 1)
+
+        if slot == 2 * tiles - 1:
+
+            @pl.when(jnp.logical_or(jnp.logical_and(i > 1, i < last), i == last))
+            def _():
+                pump_t(jnp.where(i == last, last, i - 1))
+
     def pump(i, slot):
         if slot == 0:
             front(i + 1, 2)
-        if slot == 1:
+        if slot == min(2, 2 * tiles - 1):
             front(i + 1, 3)
         if slot == tiles:
             back(i + 1, 0)
         if slot == 2 * tiles - 1:
             back(i + 1, 1)
-
-            @pl.when(i + 1 < seq_n)
-            def _():
-                pump_t(i + 1)
-
         if slot == 2 * tiles:
             back(i + 1, 2)
             front(i + 2, 0)
         if slot == slots - 1:
             back(i + 1, 3)
             front(i + 2, 1)
+        text_front(i, slot)
 
     def project(j, t, b):
         at = pl.ds(t * tile, tile)
@@ -493,49 +505,50 @@
     text_rows = txt.shape[2]
     count = seq_n * text_rows
 
-    def copy_o(core, branch):
+    def copy_o(core, t, own):
+        to = (x + t) % ten_n
+        branch = core if own == 0 else 1 - core
         at = pl.ds(aligned(branch, out_rows), out_rows)
-        return remote(
-            attf.at[core, :, at], attf.at[core, :, at], send_o.at[branch], recv_o.at[branch], cfg=other
-        )
-
-    for own in range(2):
+        place = attf.at[core, to, at]
+        return remote(place, place, send_o.at[t, own], recv_o.at[t, own], cfg=other)
+
+    def text(t, own):
+        to = (x + t) % ten_n
+        here = pl.ds(aligned(to, out_rows), out_rows)
         branch = c if own == 0 else other
         source = txt if own == 0 else txo
         base = aligned(c, mine) if own == 0 else 0
         valid = lax.broadcasted_iota(jnp.int32, (1, count), 1).astype(F32) < lens[branch, 0:1, :]
         ahead = {}
-        for step_n in range(heads + 2):
-            if step_n < heads:
-                src = pl.ds(pl.multiple_of(base + step_n * HEAD_DIM, HEAD_DIM), HEAD_DIM)
+        for n in range(heads + 2):
+            if n < heads:
+                src = pl.ds(pl.multiple_of(base + n * HEAD_DIM, HEAD_DIM), HEAD_DIM)
                 raw = source[:, 0, :, src].reshape(count, HEAD_DIM).astype(F32)
                 inverse = lax.rsqrt(jnp.mean(raw * raw, axis=-1, keepdims=True) + 1e-06)
                 keys = (raw * inverse * gains[1:2, :]).astype(BF16)
-                ahead[step_n] = lax.dot_general(
-                    qbuf[branch * heads + step_n], keys, (((1,), (1,)), ((), ())), preferred_element_type=F32
+                ahead[n] = lax.dot_general(
+                    qbuf[branch * heads + n, here, :],
+                    keys,
+                    (((1,), (1,)), ((), ())),
+                    preferred_element_type=F32,
                 )
-            if step_n < 2:
+            if n < 2:
                 continue
-            h = step_n - 2
-            n = branch * heads + h
+            h = n - 2
+            row = branch * heads + h
             src = pl.ds(pl.multiple_of(base + h * HEAD_DIM, HEAD_DIM), HEAD_DIM)
             values = source[:, 1, :, src].reshape(count, HEAD_DIM)
             expo = jnp.where(valid, jnp.exp2(ahead.pop(h)), 0.0)
-            total = jnp.sum(lsum[n], axis=-1, keepdims=True) + jnp.sum(
+            total = jnp.sum(lsum[row, here, :], axis=-1, keepdims=True) + jnp.sum(
                 expo, axis=-1, keepdims=True
             )
-            mixed = acc[n] + jnp.dot(expo.astype(BF16), values, preferred_element_type=F32)
-            result = (mixed * (1.0 / total)).astype(BF16)
-            for t in range(ten_n):
-                attf[c, t, pl.ds(aligned(branch, out_rows), out_rows), h * HEAD_DIM : (h + 1) * HEAD_DIM] = (
-                    result[t * out_rows : (t + 1) * out_rows]
-                )
-
-        copy_o(c, branch).start()
-
-    out_local.wait()
-    copy_o(other, other).wait_recv()
-    copy_o(other, c).wait_recv()
+            mixed = acc[row, here, :] + jnp.dot(
+                expo.astype(BF16), values, preferred_element_type=F32
+            )
+            attf[
+                c, to, pl.ds(aligned(branch, out_rows), out_rows), h * HEAD_DIM : (h + 1) * HEAD_DIM
+            ] = (mixed * (1.0 / total)).astype(BF16)
+        copy_o(c, t, own).start()
 
     out_tile = 256 if out_cols % 256 == 0 else 128
     out_tiles = out_cols // out_tile
@@ -558,13 +571,21 @@
             + y[out_rows:] * ((1.0 - strength) * modulation[2, 1:2, at_gate])
         )
 
-    for t in range(1, ten_n):
+    turn = list(range(1, ten_n)) + [0]
+    text(turn[0], 0)
+    text(turn[0], 1)
+    out_local.wait()
+    for n, t in enumerate(turn):
+        if n + 1 < ten_n:
+            text(turn[n + 1], 0)
+        copy_o(other, t, 0).wait_recv()
+        copy_o(other, t, 1).wait_recv()
         for k in range(out_tiles):
             part[t, k] = out_block(t, k).astype(BF16)
-            copy_r(t, k).start()
-
-    for k in range(out_tiles):
-        part[0, k] = out_block(0, k).astype(BF16)
+            if t > 0:
+                copy_r(t, k).start()
+        if n + 1 < ten_n:
+            text(turn[n + 1], 1)
 
     for k in range(out_tiles):
         total = part[0, k].astype(F32)
@@ -576,8 +597,9 @@
     for j in range(3):
         w_copy[j].wait_send()
     copy_l(c).wait_send()
-    for b in range(2):
-        copy_o(c, b).wait_send()
+    for t in range(ten_n):
+        for own in range(2):
+            copy_o(c, t, own).wait_send()
     for t in range(1, ten_n):
         for k in range(out_tiles):
             copy_r(t, k).wait_send()
@@ -673,8 +695,8 @@
             dma((3,)),
             dma((1,)),
             dma((1,)),
-            dma((2,)),
-            dma((2,)),
+            dma((ten_n, 2)),
+            dma((ten_n, 2)),
             dma((ten_n, out_tiles)),
             dma((ten_n, out_tiles)),
             dma((8,)),

time: 76.6 us -> 75.1 us (0.980)
  Pallas kernels: 71.4 us -> 69.9 us
    pallas_call x1, Pallas kernels: 71.4 us -> 69.9 us  [local(): pl.pallas_call(functools.partial(kernel, seq_n, ten_n), out_shape=jax.Sha...]
where the time goes in v3:
time: 75.1 us; the launch traced here: 74.8 us
  Pallas kernels  69.9 us (93%)
  local copies, waits for them, and re-layouts  2.95 us (4%)
  between operations  1.31 us (2%)
    pallas_call x1, Pallas kernels, local(): pl.pallas_call(functools.partial(kernel, seq_n, ten_n), out_shape=jax.Sha...  69.9 us
    unnamed x1, local copies, waits for them, and re-layouts  1.77 us

profile of v3, /device:TPU:0, one launch (start us, length us, event | category | flops | bytes accessed | tf_op | source)
XLA Modules:
  0.0 74.8 jit_solution(4013981703821420580)
XLA Ops:
  1.3 0.7 convert_element_type.8
  2.0 0.6 broadcast_in_dim.9.lens_in
  2.6 0.6 pad.4.pos_in
  3.2 69.9 %shard_map.118 = bf16[128,1536]{1,0:T(8,128)(2,1)} custom-call(bf16[256,3072]{1,0:T(8,128)(2,1)} %latent.1, bf16[16,256]{1,0:T(8,128)(2,1)} %pad.4.pos_in, bf16[1,2,16,1536]{3,2,1,0:T(8,128)(2,1)} %text_kv.1, f32[8,64]{1,0:T(8,128)} %broadcast_in_dim.9.lens_in, f32[3,2,3072]{2,1,0:T(2,128)} %modulation.1, bf16[3,1536,1536]{2,1,0:T(8,128)(2,1)} %w_qkv.1, ...), custom_call_target="tpu_custom_call" | custom-call | tf_op jit(solution)/shard_map/pallas_call | solution.py:646
  73.1 1.8 %copy.16 = bf16[128,1536]{1,0:T(8,128)(2,1)} copy(bf16[128,1536]{1,0:T(8,128)(2,1)} %shard_map.118) | data formatting | bytes 786432

commit v4 on v3

--- a/solution.py
+++ b/solution.py
@@ -164,9 +164,7 @@
         for j in range(3)
     ]
     lat_local = pltpu.make_async_copy(latent, lat.at[z], loc.at[3])
-    pos_local = pltpu.make_async_copy(pos_in, pos.at[z], loc.at[4])
     txt_local = pltpu.make_async_copy(text_kv.at[0], txt.at[z], loc.at[5])
-    len_local = pltpu.make_async_copy(lens_in, lens.at[c], loc.at[6])
     out_local = pltpu.make_async_copy(w_out, wout, loc.at[7])
 
     def strip_of(core, s, ten):
@@ -197,7 +195,7 @@
         return remote(lat.at[o, at], lat.at[o, at], send_c.at[o, s], recv_c.at[o, s], cfg=other)
 
     def first_p(d):
-        return remote(pos_in, pos.at[z], send_p.at[z, up(d)], recv_p.at[z], seq=z + d)
+        return copy_p(z, d)
 
     def copy_p(o, d):
         return remote(pos.at[o], pos.at[o], send_p.at[o, up(d)], recv_p.at[o], seq=z + d)
@@ -217,15 +215,9 @@
         return remote(txt.at[o, :, :, cols_of(other)], txo.at[o], send_u.at[o], recv_u.at[o], cfg=other)
 
     def copy_l(core):
-        return remote(lens_in, lens.at[core], send_l.at[0], recv_l.at[0], cfg=other)
-
-    for j in range(3):
-        w_local[j].start()
+        return remote(lens.at[core], lens.at[core], send_l.at[0], recv_l.at[0], cfg=other)
+
     lat_local.start()
-    pos_local.start()
-    txt_local.start()
-    len_local.start()
-    out_local.start()
 
     barrier = pltpu.get_barrier_semaphore()
     for d in (1, -1):
@@ -240,15 +232,42 @@
             barrier, inc=1, device_id={"tensor": (x + t) % ten_n}, device_id_type=MESH
         )
 
-    def normalize(at):
-        value = lat[z, at, :].astype(F32)
-        center = value - jnp.mean(value, axis=-1, keepdims=True)
-        normed = center * lax.rsqrt(jnp.mean(center * center, axis=-1, keepdims=True) + 1e-06)
-        lat[z, at, :] = normed.astype(BF16)
-
+    def normalize(core, ten):
+        spots = [strip_of(core, s, ten) for s in range(subs)]
+        lanes = [slice(k * HEAD_DIM, (k + 1) * HEAD_DIM) for k in range(width // HEAD_DIM)]
+
+        def mean_of(body):
+            means = []
+            for at in spots:
+                total = body(at, lanes[0], len(means))
+                for lane in lanes[1:]:
+                    total = total + body(at, lane, len(means))
+                means.append(jnp.sum(total, axis=-1, keepdims=True) * (1.0 / width))
+            return means
+
+        means = mean_of(lambda at, lane, n: lat[z, at, lane].astype(F32))
+
+        def squared(at, lane, n):
+            center = lat[z, at, lane].astype(F32) - means[n]
+            return center * center
+
+        inverses = [lax.rsqrt(power + 1e-06) for power in mean_of(squared)]
+        for n, at in enumerate(spots):
+            for lane in lanes:
+                lat[z, at, lane] = (
+                    (lat[z, at, lane].astype(F32) - means[n]) * inverses[n]
+                ).astype(BF16)
+
+    pos[z] = jnp.concatenate(
+        [pos_in[...].astype(F32), jnp.zeros((16 - pos_in.shape[0], rows), F32)]
+    ).astype(BF16)
+    lens[c] = jnp.broadcast_to(lens_in[0:1, 0:1].astype(F32), lens.shape[1:])
     lat_local.wait()
-    for s in range(subs):
-        normalize(strip_of(c, s, x))
+    for j in range(3):
+        w_local[j].start()
+    txt_local.start()
+    out_local.start()
+    normalize(c, x)
 
     sides = jnp.where(z > 0, 1, 0) + jnp.where(z < seq_n - 1, 1, 0)
     pl.semaphore_wait(barrier, ten_n + sides)
@@ -266,15 +285,9 @@
     copy_l(c).start()
     first_u().start()
 
-    for t in range(1, ten_n):
-        for s in range(subs):
-            normalize(strip_of(c, s, (x + t) % ten_n))
-
-    @pl.loop(0, half_rows // STRIP, unroll=4)
-    def _(r):
-        normalize(pl.ds(aligned(other * (half_rows // STRIP) + r, STRIP), STRIP))
-
-    pos_local.wait()
+    @pl.loop(1, 2 * ten_n)
+    def _(g):
+        normalize(jnp.where(g < ten_n, c, other), (x + g) % ten_n)
 
     def pump_a(k, s):
         for d in (1, -1):
@@ -341,17 +354,23 @@
                 def _():
                     first_t(d).start()
 
-        if slot == 1 and last > 1:
+        if slot == 0 and last > 1:
 
             @pl.when(i == last)
             def _():
                 pump_t(last - 1)
 
+        if slot == tiles:
+
+            @pl.when(jnp.logical_and(i > 1, i < last))
+            def _():
+                pump_t(i - 1)
+
         if slot == 2 * tiles - 1:
 
-            @pl.when(jnp.logical_or(jnp.logical_and(i > 1, i < last), i == last))
+            @pl.when(i == last)
             def _():
-                pump_t(jnp.where(i == last, last, i - 1))
+                pump_t(last)
 
     def pump(i, slot):
         if slot == 0:
@@ -495,7 +514,6 @@
         step(i, False)
 
     txt_local.wait()
-    len_local.wait()
     copy_l(other).wait_recv()
 
     @pl.loop(0, seq_n)
@@ -580,19 +598,15 @@
             text(turn[n + 1], 0)
         copy_o(other, t, 0).wait_recv()
         copy_o(other, t, 1).wait_recv()
+        block = out_block(t, 0)
         for k in range(out_tiles):
-            part[t, k] = out_block(t, k).astype(BF16)
+            later = out_block(t, k + 1) if k + 1 < out_tiles else None
+            part[t, k] = block.astype(BF16)
             if t > 0:
                 copy_r(t, k).start()
+            block = later
         if n + 1 < ten_n:
             text(turn[n + 1], 1)
-
-    for k in range(out_tiles):
-        total = part[0, k].astype(F32)
-        for t in range(1, ten_n):
-            copy_r(t, k).wait_recv()
-            total = total + got[t, k].astype(F32)
-        out[:, k * out_tile : (k + 1) * out_tile] = total.astype(BF16)
 
     for j in range(3):
         w_copy[j].wait_send()
@@ -600,9 +614,6 @@
     for t in range(ten_n):
         for own in range(2):
             copy_o(c, t, own).wait_send()
-    for t in range(1, ten_n):
-        for k in range(out_tiles):
-            copy_r(t, k).wait_send()
 
     @pl.loop(0, seq_n)
     def _(o):
@@ -624,6 +635,23 @@
                 copy_t(o, d).wait_send()
                 for s in range(subs):
                     copy_a(o, s, d).wait_send()
+
+    def emit(k):
+        return pltpu.make_async_copy(
+            part.at[0, k], out.at[:, pl.ds(k * out_tile, out_tile)], loc.at[8 + k]
+        )
+
+    for k in range(out_tiles):
+        total = part[0, k].astype(F32)
+        for t in range(1, ten_n):
+            copy_r(t, k).wait_recv()
+            total = total + got[t, k].astype(F32)
+        part[0, k] = total.astype(BF16)
+        emit(k).start()
+    for k in range(out_tiles):
+        for t in range(1, ten_n):
+            copy_r(t, k).wait_send()
+        emit(k).wait()
 
 
 def local(
@@ -638,8 +666,6 @@
     out_tile = 256 if out_cols % 256 == 0 else 128
     out_tiles = out_cols // out_tile
     subs = rows // (2 * ten_n * STRIP)
-    pos_in = jnp.pad(positions.astype(BF16), ((0, 13), (0, 0)))
-    lens = jnp.broadcast_to(text_len.astype(F32)[None, :], (8, seq_n * text_dev))
     any_space = pl.BlockSpec(memory_space=pl.ANY)
     vmem = pl.BlockSpec(memory_space=pltpu.VMEM)
     dma = pltpu.SemaphoreType.DMA
@@ -648,9 +674,9 @@
         out_shape=jax.ShapeDtypeStruct((out_rows, out_cols), BF16),
         in_specs=[
             any_space,
+            vmem,
             any_space,
-            any_space,
-            any_space,
+            vmem,
             vmem,
             any_space,
             vmem,
@@ -660,7 +686,7 @@
             vmem,
             vmem,
         ],
-        out_specs=vmem,
+        out_specs=any_space,
         scratch_shapes=[
             pltpu.VMEM((seq_n, rows, width), BF16),
             pltpu.VMEM((seq_n, 16, rows), BF16),
@@ -699,16 +725,16 @@
             dma((ten_n, 2)),
             dma((ten_n, out_tiles)),
             dma((ten_n, out_tiles)),
-            dma((8,)),
+            dma((8 + out_tiles,)),
         ],
         compiler_params=pltpu.CompilerParams(
             collective_id=0, has_side_effects=True, vmem_limit_bytes=64 * 1024 * 1024 - 65536
         ),
     )(
         latent,
-        pos_in,
+        positions,
         text_kv,
-        lens,
+        text_len.reshape(1, 1),
         modulation,
         w_qkv,
         norm_gains,

time: 75.1 us -> 69 us (0.919)
  Pallas kernels: 69.9 us -> 65.7 us
  local copies, waits for them, and re-layouts: 2.95 us -> 1.77 us
    pallas_call x1, Pallas kernels: 69.9 us -> 65.7 us  [local(): pl.pallas_call(functools.partial(kernel, seq_n, ten_n), out_shape=jax.Sha...]
where the time goes in v4:
time: 69 us; the launch traced here: 68.8 us
  Pallas kernels  65.7 us (95%)
  local copies, waits for them, and re-layouts  1.77 us (3%)
  between operations  1.31 us (2%)
    pallas_call x1, Pallas kernels, local(): pl.pallas_call(functools.partial(kernel, seq_n, ten_n), out_shape=jax.Sha...  65.7 us
    unnamed x1, local copies, waits for them, and re-layouts  1.77 us

profile of v4, /device:TPU:0, one launch (start us, length us, event | category | flops | bytes accessed | tf_op | source)
XLA Modules:
  0.0 68.8 jit_solution(4729419763522958605)
XLA Ops:
  1.3 65.7 %shard_map.118 = bf16[128,1536]{1,0:T(8,128)(2,1)} custom-call(bf16[256,3072]{1,0:T(8,128)(2,1)} %latent.1, s32[3,256]{1,0:T(4,128)} %pos_in.1, bf16[1,2,16,1536]{3,2,1,0:T(8,128)(2,1)} %text_kv.1, s32[1,1]{1,0:T(1,128)} %bitcast.2.lens_in, f32[3,2,3072]{2,1,0:T(2,128)} %modulation.1, bf16[3,1536,1536]{2,1,0:T(8,128)(2,1)} %w_qkv.1, f32[2,128]{1,0:T(2,128)} %gains.1, ...), custom_call_target="tpu_custom_call" | custom-call | tf_op jit(solution)/shard_map/pallas_call | solution.py:672
  67.0 1.8 %copy.16 = bf16[128,1536]{1,0:T(8,128)(2,1)} copy(bf16[128,1536]{1,0:T(8,128)(2,1)} %shard_map.118) | data formatting | bytes 786432

commit v5 on v4

--- a/solution.py
+++ b/solution.py
@@ -183,12 +183,12 @@
     def copy_b(o, s, t):
         at = strip_of(c, s, x)
         to = (x + t) % ten_n
-        return remote(lat.at[o, at], lat.at[o, at], send_b.at[o, s, t], recv_b.at[o, s, t], tensor=to)
+        return remote(lat.at[o, at], lat.at[o, at], send_b.at[o, s, t - 1], recv_b.at[o, s, t - 1], tensor=to)
 
     def arrived_b(o, s, t):
         source = (x + ten_n - t) % ten_n
         at = strip_of(c, s, source)
-        return remote(lat.at[o, at], lat.at[o, at], send_b.at[o, s, t], recv_b.at[o, s, t], tensor=source)
+        return remote(lat.at[o, at], lat.at[o, at], send_b.at[o, s, t - 1], recv_b.at[o, s, t - 1], tensor=source)
 
     def copy_c(o, s, core):
         at = band_of(core, s)
@@ -497,7 +497,7 @@
                 if j > 0:
                     pump(i, (j - 1) * tiles + t)
                     continue
-                if t == max(tiles - 2, 0):
+                if t == 0:
                     front(1, 0)
                 if t == tiles - 1:
                     front(1, 1)
@@ -580,7 +580,7 @@
 
     def out_block(t, k):
         to = (x + t) % ten_n
-        at = pl.ds(k * out_tile, out_tile)
+        at = pl.ds(aligned(k, out_tile), out_tile)
         y = jnp.dot(attf[0, to], wout[0:mine, at], preferred_element_type=F32)
         y = y + jnp.dot(attf[1, to], wout[mine : 2 * mine, at], preferred_element_type=F32)
         at_gate = pl.ds(pl.multiple_of(c * out_cols + k * out_tile, out_tile), out_tile)
@@ -598,13 +598,16 @@
             text(turn[n + 1], 0)
         copy_o(other, t, 0).wait_recv()
         copy_o(other, t, 1).wait_recv()
-        block = out_block(t, 0)
-        for k in range(out_tiles):
-            later = out_block(t, k + 1) if k + 1 < out_tiles else None
-            part[t, k] = block.astype(BF16)
-            if t > 0:
+        if t > 0:
+
+            @pl.loop(0, out_tiles)
+            def _(k):
+                part[t, k] = out_block(t, k).astype(BF16)
                 copy_r(t, k).start()
-            block = later
+
+        else:
+            for k in range(out_tiles):
+                part[t, k] = out_block(t, k).astype(BF16)
         if n + 1 < ten_n:
             text(turn[n + 1], 1)
 
@@ -707,8 +710,8 @@
             pltpu.VMEM((ten_n, out_tiles, out_rows, out_tile), BF16),
             dma((seq_n, subs, 2)),
             dma((seq_n, subs)),
-            dma((seq_n, subs, ten_n)),
-            dma((seq_n, subs, ten_n)),
+            dma((seq_n, subs, max(ten_n - 1, 1))),
+            dma((seq_n, subs, max(ten_n - 1, 1))),
             dma((seq_n, subs)),
             dma((seq_n, subs)),
             dma((seq_n, 2)),

time: 69 us -> 67.6 us (0.980)
  Pallas kernels: 65.7 us -> 64.3 us
    pallas_call x1, Pallas kernels: 65.7 us -> 64.3 us  [local(): pl.pallas_call(functools.partial(kernel, seq_n, ten_n), out_shape=jax.Sha...]
where the time goes in v5:
time: 67.6 us; the launch traced here: 67.4 us
  Pallas kernels  64.3 us (95%)
  local copies, waits for them, and re-layouts  1.77 us (3%)
  between operations  1.31 us (2%)
    pallas_call x1, Pallas kernels, local(): pl.pallas_call(functools.partial(kernel, seq_n, ten_n), out_shape=jax.Sha...  64.3 us
    unnamed x1, local copies, waits for them, and re-layouts  1.77 us

profile of v5, /device:TPU:0, one launch (start us, length us, event | category | flops | bytes accessed | tf_op | source)
XLA Modules:
  0.0 67.4 jit_solution(11643524011564744902)
XLA Ops:
  1.3 64.3 %shard_map.118 = bf16[128,1536]{1,0:T(8,128)(2,1)} custom-call(bf16[256,3072]{1,0:T(8,128)(2,1)} %latent.1, s32[3,256]{1,0:T(4,128)} %pos_in.1, bf16[1,2,16,1536]{3,2,1,0:T(8,128)(2,1)} %text_kv.1, s32[1,1]{1,0:T(1,128)} %bitcast.2.lens_in, f32[3,2,3072]{2,1,0:T(2,128)} %modulation.1, bf16[3,1536,1536]{2,1,0:T(8,128)(2,1)} %w_qkv.1, f32[2,128]{1,0:T(2,128)} %gains.1, ...), custom_call_target="tpu_custom_call" | custom-call | tf_op jit(solution)/shard_map/pallas_call | solution.py:675
  65.6 1.8 %copy.16 = bf16[128,1536]{1,0:T(8,128)(2,1)} copy(bf16[128,1536]{1,0:T(8,128)(2,1)} %shard_map.118) | data formatting | bytes 786432

commit v6 on v5

--- a/solution.py
+++ b/solution.py
@@ -178,21 +178,29 @@
 
     def copy_a(o, s, d):
         at = strip_of(c, s, x)
-        return remote(lat.at[o, at], lat.at[o, at], send_a.at[o, s, up(d)], recv_a.at[o, s], seq=z + d)
+        return remote(lat.at[o, at], lat.at[o, at], send_a.at[o, up(d)], recv_a.at[o, s], seq=z + d)
 
     def copy_b(o, s, t):
         at = strip_of(c, s, x)
         to = (x + t) % ten_n
-        return remote(lat.at[o, at], lat.at[o, at], send_b.at[o, s, t - 1], recv_b.at[o, s, t - 1], tensor=to)
+        return remote(lat.at[o, at], lat.at[o, at], send_b.at[o, t - 1], recv_b.at[o, s, t - 1], tensor=to)
 
     def arrived_b(o, s, t):
         source = (x + ten_n - t) % ten_n
         at = strip_of(c, s, source)
-        return remote(lat.at[o, at], lat.at[o, at], send_b.at[o, s, t - 1], recv_b.at[o, s, t - 1], tensor=source)
+        return remote(lat.at[o, at], lat.at[o, at], send_b.at[o, t - 1], recv_b.at[o, s, t - 1], tensor=source)
 
     def copy_c(o, s, core):
         at = band_of(core, s)
-        return remote(lat.at[o, at], lat.at[o, at], send_c.at[o, s], recv_c.at[o, s], cfg=other)
+        return remote(lat.at[o, at], lat.at[o, at], send_c.at[o], recv_c.at[o], cfg=other)
+
+    def sent_rows(o, count, sem):
+        at = pl.ds(0, count)
+        return remote(lat.at[o, at], lat.at[o, at], sem, recv_c.at[o], cfg=other)
+
+    def half_of(o, core):
+        at = pl.ds(aligned(core, half_rows), half_rows)
+        return remote(lat.at[o, at], lat.at[o, at], send_c.at[o], recv_c.at[o], cfg=other)
 
     def first_p(d):
         return copy_p(z, d)
@@ -479,8 +487,7 @@
         tables(o, first)
         modulate(o, c)
         if not first:
-            for s in range(subs):
-                copy_c(o, s, other).wait_recv()
+            half_of(o, other).wait_recv()
         modulate(o, other)
 
         pending = None
@@ -573,7 +580,7 @@
 
     def copy_r(t, k):
         return remote(
-            part.at[t, k], got.at[t, k], send_r.at[t, k], recv_r.at[t, k], tensor=(x + t) % ten_n
+            part.at[t, k], got.at[t, k], send_r.at[t - 1], recv_r.at[t - 1, k], tensor=(x + t) % ten_n
         )
 
     strength = guide[0:1, 0:1]
@@ -624,10 +631,9 @@
 
         @pl.when(o != z)
         def _():
-            for s in range(subs):
-                for t in range(1, ten_n):
-                    copy_b(o, s, t).wait_send()
-                copy_c(o, s, c).wait_send()
+            for t in range(1, ten_n):
+                sent_rows(o, subs * STRIP, send_b.at[o, t - 1]).wait_send()
+            sent_rows(o, half_rows, send_c.at[o]).wait_send()
 
         for d in (1, -1):
             ahead = jnp.logical_or(o == z, d * (z - o) > 0)
@@ -636,8 +642,7 @@
             def _():
                 copy_p(o, d).wait_send()
                 copy_t(o, d).wait_send()
-                for s in range(subs):
-                    copy_a(o, s, d).wait_send()
+                sent_rows(o, subs * STRIP, send_a.at[o, up(d)]).wait_send()
 
     def emit(k):
         return pltpu.make_async_copy(
@@ -651,9 +656,11 @@
             total = total + got[t, k].astype(F32)
         part[0, k] = total.astype(BF16)
         emit(k).start()
+    for t in range(1, ten_n):
+        remote(
+            part.at[t], got.at[t], send_r.at[t - 1], recv_r.at[t - 1, 0], tensor=(x + t) % ten_n
+        ).wait_send()
     for k in range(out_tiles):
-        for t in range(1, ten_n):
-            copy_r(t, k).wait_send()
         emit(k).wait()
 
 
@@ -708,12 +715,12 @@
             pltpu.VMEM((2, ten_n, 2 * out_rows, mine), BF16),
             pltpu.VMEM((ten_n, out_tiles, out_rows, out_tile), BF16),
             pltpu.VMEM((ten_n, out_tiles, out_rows, out_tile), BF16),
-            dma((seq_n, subs, 2)),
+            dma((seq_n, 2)),
             dma((seq_n, subs)),
+            dma((seq_n, max(ten_n - 1, 1))),
             dma((seq_n, subs, max(ten_n - 1, 1))),
-            dma((seq_n, subs, max(ten_n - 1, 1))),
-            dma((seq_n, subs)),
-            dma((seq_n, subs)),
+            dma((seq_n,)),
+            dma((seq_n,)),
             dma((seq_n, 2)),
             dma((seq_n,)),
             dma((seq_n, 2)),
@@ -726,8 +733,8 @@
             dma((1,)),
             dma((ten_n, 2)),
             dma((ten_n, 2)),
-            dma((ten_n, out_tiles)),
-            dma((ten_n, out_tiles)),
+            dma((max(ten_n - 1, 1),)),
+            dma((max(ten_n - 1, 1), out_tiles)),
             dma((8 + out_tiles,)),
         ],
         compiler_params=pltpu.CompilerParams(

time: 67.6 us -> 66.9 us (0.990)
  Pallas kernels: 64.3 us -> 63.6 us
    pallas_call x1, Pallas kernels: 64.3 us -> 63.6 us  [local(): pl.pallas_call(functools.partial(kernel, seq_n, ten_n), out_shape=jax.Sha...]
where the time goes in v6:
time: 66.9 us; the launch traced here: 66.7 us
  Pallas kernels  63.6 us (95%)
  local copies, waits for them, and re-layouts  1.77 us (3%)
  between operations  1.31 us (2%)
    pallas_call x1, Pallas kernels, local(): pl.pallas_call(functools.partial(kernel, seq_n, ten_n), out_shape=jax.Sha...  63.6 us
    unnamed x1, local copies, waits for them, and re-layouts  1.77 us

profile of v6, /device:TPU:0, one launch (start us, length us, event | category | flops | bytes accessed | tf_op | source)
XLA Modules:
  0.0 66.7 jit_solution(3691641429789527728)
XLA Ops:
  1.3 63.6 %shard_map.118 = bf16[128,1536]{1,0:T(8,128)(2,1)} custom-call(bf16[256,3072]{1,0:T(8,128)(2,1)} %latent.1, s32[3,256]{1,0:T(4,128)} %pos_in.1, bf16[1,2,16,1536]{3,2,1,0:T(8,128)(2,1)} %text_kv.1, s32[1,1]{1,0:T(1,128)} %bitcast.2.lens_in, f32[3,2,3072]{2,1,0:T(2,128)} %modulation.1, bf16[3,1536,1536]{2,1,0:T(8,128)(2,1)} %w_qkv.1, f32[2,128]{1,0:T(2,128)} %gains.1, ...), custom_call_target="tpu_custom_call" | custom-call | tf_op jit(solution)/shard_map/pallas_call | solution.py:682
  64.9 1.8 %copy.16 = bf16[128,1536]{1,0:T(8,128)(2,1)} copy(bf16[128,1536]{1,0:T(8,128)(2,1)} %shard_map.118) | data formatting | bytes 786432
